TPU v7x, 256 devices: a whole 4x4x8 slice. The times are simulated.
256 devices in a mesh: gx: 8 (over z_lo, core), gy: 32 (over z_hi, y, x).
Axes of the slice: x: 4, y: 4, z: 8 (z_hi: 2, z_lo: 4; z = z_hi * 4 + z_lo), core: 2. Of those that a mesh axis runs over, the one named last changes fastest.
Arguments:
- density: float32 [128, 512, 256], P('gx', 'gy'), may hold values from 0.5 to 2
- momentum: float32 [3, 128, 512, 256], P(None, 'gx', 'gy'), may hold values from -3 to 3
- energy: float32 [128, 512, 256], P('gx', 'gy'), may hold values from 1 to 3
- parcel_mass: float32 [2097152], P(('gx', 'gy')), may hold values from 0.2 to 2
- droplet_velocity: float32 [3, 2097152], P(None, ('gx', 'gy')), may hold values from -4 to 4
- parcel_temp: float32 [2097152], P(('gx', 'gy')), may hold values from 0.1 to 4
- parcel_cell: int32 [3, 2097152], P(None, ('gx', 'gy')), may hold values from 0 to 511, as said below
- parcel_count: int32 [256], P(('gx', 'gy')), may hold values from 2048 to 8192, as said below
Outputs:
- updated_fluid_density: float32 [128, 512, 256], P('gx', 'gy')
- updated_fluid_impulse: float32 [3, 128, 512, 256], P(None, 'gx', 'gy')
- energy_out: float32 [128, 512, 256], P('gx', 'gy')
- moved_state: float32 [5, 2621440], P(None, ('gx', 'gy'))
- moved_cell: int32 [3, 2621440], P(None, ('gx', 'gy'))
- time_step: float32 [], replicated
Inputs may be any that keep to these rules, and one draw needn't show every extreme that they name: `parcel_cell`: each row of device d lies in d's block of 16 x 16 x 256 cells or in the layer of cells just beyond one of its four side faces inside the grid, never beyond an edge. Among the live rows of one device at most 512 lie beyond any one face; on every device some face along each of the two axes has exactly 512. `parcel_count`: some devices are full.
All inputs are finite; a program needn't handle non-finite values.
Results may differ from a plain program's by a relative error of at most 0.0003.
Values sent between devices are 32-bit elements; how exact they have to be, the bound alone decides.
A program may use at most 192 MiB of HBM per device.

v0:
```python
import jax
import jax.numpy as jnp
from jax import lax
from jax.sharding import Mesh
from jax.sharding import PartitionSpec as P

GX = ("gx_0", "gx_1")
GY = ("gy_0", "gy_1", "gy_2")
GX_GY = ("gx_0", "gx_1", "gy_0", "gy_1", "gy_2")


ADIABATIC_INDEX = 1.4
KICK = 0.25
COURANT = 0.4
SHRINK = 0.5


def with_halo(cells, sides, width):
    for axis, dim in sides:
        count = lax.axis_size(axis)
        ends = count - 1
        head = lax.slice_in_dim(cells, 0, width, axis=dim)
        tail = lax.slice_in_dim(cells, cells.shape[dim] - width, cells.shape[dim], axis=dim)
        cells = jnp.concatenate(
            [
                lax.ppermute(tail, axis, [(i, (i + 1) % count) for i in range(ends)]),
                cells,
                lax.ppermute(head, axis, [((i + 1) % count, i) for i in range(ends)]),
            ],
            axis=dim,
        )
    return cells


def padded_2(shard, sides, width):
    edges = {}
    for axis, dim in sides:
        size, length = (lax.axis_size(axis), shard.shape[dim])
        up = [(i, (i + 1) % size) for i in range(size - 1)]
        last = lax.slice_in_dim(shard, length - width, length, axis=dim)
        leading = lax.slice_in_dim(shard, 0, width, axis=dim)
        edges[dim] = (
            lax.ppermute(last, axis, up),
            lax.ppermute(leading, axis, [(b, a) for a, b in up]),
        )
    done = []
    for _, dim in sides:
        low, high = edges[dim]
        around = [(width, width) if d in done else (0, 0) for d in range(shard.ndim)]
        shard = jnp.concatenate([jnp.pad(low, around), shard, jnp.pad(high, around)], axis=dim)
        done.append(dim)
    return shard


def over_axes(shard, axes):
    for axis in axes:
        shard = lax.pmax(shard, axis)
    return shard


def gather_coupling_feedback(boiled_off_amount, ambient_stream_speed, ambient_thermal_reading):
    specific_movement_budget = 0.5 * jnp.sum(ambient_stream_speed * ambient_stream_speed, axis=0)
    return jnp.concatenate(
        [
            boiled_off_amount[None],
            boiled_off_amount[None] * ambient_stream_speed,
            (boiled_off_amount * (ambient_thermal_reading + specific_movement_budget))[None],
        ],
        axis=0,
    )


def on_device(
    density, momentum, energy, parcel_mass, droplet_velocity, parcel_temp, parcel_cell, parcel_count
):
    cells_x, cells_y, depth_cells = density.shape
    row_total = parcel_mass.shape[0]
    capacity = row_total // 16
    anchor_x = lax.axis_index(GX) * cells_x
    anchor_y = lax.axis_index(GY) * cells_y
    live = jnp.arange(row_total, dtype=jnp.int32) < parcel_count[0]
    boiled_off_amount = jnp.where(
        live, parcel_mass * jax.nn.sigmoid(2.0 * (parcel_temp - 2.0)), 0.0
    )
    sources = gather_coupling_feedback(boiled_off_amount, droplet_velocity, parcel_temp)
    local_x = parcel_cell[0] - anchor_x
    local_y = parcel_cell[1] - anchor_y
    heading = jnp.where(
        local_x < 0,
        0,
        jnp.where(
            local_x >= cells_x, 1, jnp.where(local_y < 0, 2, jnp.where(local_y >= cells_y, 3, 4))
        ),
    )
    heading = jnp.where(live, heading, 5).astype(jnp.int32)
    onehot = (heading[:, None] == jnp.arange(4, dtype=jnp.int32)[None]).astype(jnp.int32)
    earlier = jnp.cumsum(onehot, axis=0) - onehot
    rank = jnp.sum(earlier * onehot, axis=1)
    carried_records = jnp.concatenate(
        [
            (parcel_mass - SHRINK * boiled_off_amount)[None],
            droplet_velocity,
            parcel_temp[None],
            parcel_cell.astype(jnp.float32),
            boiled_off_amount[None],
        ],
        axis=0,
    )
    target = jnp.where(heading < 4, heading * capacity + rank, 4 * capacity)
    buckets = (
        jnp.zeros((9, 4 * capacity), jnp.float32)
        .at[:, target]
        .set(carried_records, mode="drop")
        .reshape(9, 4, capacity)
    )
    staying = jnp.where((heading == 4)[None], carried_records[:8], 0.0)
    block_cells = cells_x * cells_y * depth_cells
    face_x = (cells_y + 2) * depth_cells
    face_y = cells_x * depth_cells
    total_cells = block_cells + 2 * face_x + 2 * face_y
    depth_of = parcel_cell[2]
    within_x = (local_x >= 0) & (local_x < cells_x)
    within_y = (local_y >= 0) & (local_y < cells_y)
    cell_slot = jnp.where(
        within_x & within_y,
        (local_x * cells_y + local_y) * depth_cells + depth_of,
        jnp.where(
            local_x < 0,
            block_cells + (local_y + 1) * depth_cells + depth_of,
            jnp.where(
                local_x >= cells_x,
                block_cells + face_x + (local_y + 1) * depth_cells + depth_of,
                jnp.where(
                    local_y < 0,
                    block_cells + 2 * face_x + local_x * depth_cells + depth_of,
                    block_cells + 2 * face_x + face_y + local_x * depth_cells + depth_of,
                ),
            ),
        ),
    )
    cell_slot = jnp.clip(cell_slot, 0, total_cells - 1)

    def deposit_one(values):
        return jax.ops.segment_sum(values, cell_slot, num_segments=total_cells)

    flat_sums = jax.vmap(deposit_one)(sources)
    core = flat_sums[:, :block_cells].reshape(5, cells_x, cells_y, depth_cells)
    lower_x = flat_sums[:, block_cells : block_cells + face_x]
    upper_x = flat_sums[:, block_cells + face_x : block_cells + 2 * face_x]
    lower_y = flat_sums[:, block_cells + 2 * face_x : block_cells + 2 * face_x + face_y].reshape(
        5, cells_x, depth_cells
    )
    upper_y = flat_sums[:, block_cells + 2 * face_x + face_y :].reshape(5, cells_x, depth_cells)
    eight = buckets[:8]
    size_x = 5 * face_x
    faces_x = jnp.stack([lower_x.reshape(-1), upper_x.reshape(-1)])
    faces_x = jnp.concatenate(
        [faces_x, jnp.stack([eight[:, 0].reshape(-1), eight[:, 1].reshape(-1)])], axis=1
    )
    got_x = with_halo(faces_x, ((GX, 0),), 1)
    from_lower = got_x[0, :size_x].reshape(5, cells_y + 2, depth_cells)
    from_upper = got_x[3, :size_x].reshape(5, cells_y + 2, depth_cells)
    core = core.at[:, 0].add(from_lower[:, 1 : cells_y + 1])
    core = core.at[:, cells_x - 1].add(from_upper[:, 1 : cells_y + 1])
    lower_y = lower_y.at[:, 0].add(from_lower[:, 0]).at[:, cells_x - 1].add(from_upper[:, 0])
    upper_y = (
        upper_y.at[:, 0]
        .add(from_lower[:, cells_y + 1])
        .at[:, cells_x - 1]
        .add(from_upper[:, cells_y + 1])
    )
    size_y = 5 * face_y
    faces_y = jnp.stack([lower_y.reshape(-1), upper_y.reshape(-1)])
    faces_y = jnp.concatenate(
        [faces_y, jnp.stack([eight[:, 2].reshape(-1), eight[:, 3].reshape(-1)])], axis=1
    )
    got_y = with_halo(faces_y, ((GY, 0),), 1)
    core = core.at[:, :, 0].add(got_y[0, :size_y].reshape(5, cells_x, depth_cells))
    core = core.at[:, :, cells_y - 1].add(got_y[3, :size_y].reshape(5, cells_x, depth_cells))
    arrived = jnp.concatenate(
        [
            got_x[0, size_x:].reshape(8, capacity),
            got_x[3, size_x:].reshape(8, capacity),
            got_y[0, size_y:].reshape(8, capacity),
            got_y[3, size_y:].reshape(8, capacity),
        ],
        axis=1,
    )
    updated_fluid_density = density + core[0]
    energy_out = energy + core[4]
    lifted = momentum + core[1:4]
    normal_stress_field = (ADIABATIC_INDEX - 1.0) * energy_out
    padded = padded_2(normal_stress_field, ((GX, 0), (GY, 1)), 1)
    grad_x = 0.5 * (padded[2:, 1:-1] - padded[:-2, 1:-1])
    grad_y = 0.5 * (padded[1:-1, 2:] - padded[1:-1, :-2])
    deep = jnp.pad(normal_stress_field, ((0, 0), (0, 0), (1, 1)))
    grad_z = 0.5 * (deep[:, :, 2:] - deep[:, :, :-2])
    updated_fluid_impulse = lifted - KICK * jnp.stack([grad_x, grad_y, grad_z])
    ambient_stream_speed = updated_fluid_impulse / updated_fluid_density[None]
    acoustic_signal = jnp.max(jnp.abs(ambient_stream_speed), axis=0) + jnp.sqrt(
        ADIABATIC_INDEX * normal_stress_field / updated_fluid_density
    )
    fastest = over_axes(jnp.max(acoustic_signal), GX_GY)
    time_step = COURANT / fastest
    table = jnp.concatenate([staying, arrived], axis=1)
    moved_state = table[:5]
    moved_cell = table[5:].astype(jnp.int32)
    return (
        updated_fluid_density,
        updated_fluid_impulse,
        energy_out,
        moved_state,
        moved_cell,
        time_step,
    )


def solution(mesh):
    split = Mesh(mesh.devices.reshape(4, 2, 2, 4, 4), ("gx_0", "gx_1", "gy_0", "gy_1", "gy_2"))
    return jax.shard_map(
        on_device,
        mesh=split,
        in_specs=(
            P(GX, GY, None),
            P(None, GX, GY, None),
            P(GX, GY, None),
            P(GX_GY),
            P(None, GX_GY),
            P(GX_GY),
            P(None, GX_GY),
            P(GX_GY),
        ),
        out_specs=(
            P(GX, GY, None),
            P(None, GX, GY, None),
            P(GX, GY, None),
            P(None, GX_GY),
            P(None, GX_GY),
            P(),
        ),
        check_vma=False,
    )
```

profile of v0, /device:TPU:1, one launch (start us, length us, event | category | flops | bytes accessed | tf_op | source)
XLA Modules:
  0.0 276.1 jit_solution(5672505770449375735)
XLA Ops:
  9.6 2.6 copy.27
  12.5 21.1 %scatter_custom_fusion.1 = f32[9,2048]{0,1:T(8,128)S(1)} fusion(s32[8192]{0:T(1024)S(1)} %bitcast.131, f32[8192,9]{1,0:T(8,128)} %copy.27, f32[]{:T(128)} %constant.250.clone.1), kind=kCustom, calls=%fused_computation.8 | custom fusion | bytes 74240 | tf_op jit(solution)/shard_map/scatter | solution.py:113
  34.9 2.7 copy.23
  37.5 61.0 %scatter_custom_fusion = f32[5,82944]{0,1:T(8,128)} fusion(s32[8192]{0:T(1024)S(1)} %bitcast.132, f32[8192,5]{1,0:T(8,128)} %copy.23, f32[]{:T(128)} %constant.250.clone.1), kind=kCustom, calls=%fused_computation.2 | custom fusion | flops 40960 | bytes 1659392 | tf_op jit(solution)/shard_map/vmap()/scatter-add | solution.py:144
  98.5 4.1 %fusion.34 = (f32[5,4608]{0,1:T(8,128)}, f32[5,4608]{0,1:T(8,128)S(1)}) fusion(f32[5,82944]{0,1:T(8,128)} %scatter_custom_fusion), kind=kLoop, calls=%fused_computation.103 | loop fusion | bytes 368640 | tf_op jit(solution)/shard_map/slice | solution.py:148
  102.6 2.4 copy.25
  107.0 4.9 %collective-permute-start = (f32[1,27136]{1,0:T(1,128)}, f32[1,27136]{1,0:T(1,128)}, u32[]{:S(2)}, u32[]{:S(2)}) collective-permute-start(f32[1,27136]{1,0:T(1,128)} %get-tuple-element.127), channel_id=1, source_target_pairs={{0,32},{32,64},{64,96},{96,128},{128,160},{160,192},{192,224},{1,3... | collective-permute-start | bytes 325640 | tf_op jit(solution)/shard_map/ppermute | solution.py:26
  114.9 4.4 %fusion.33 = (f32[5,4096]{0,1:T(8,128)}, f32[5,4096]{0,1:T(8,128)}) fusion(f32[5,82944]{0,1:T(8,128)} %scatter_custom_fusion), kind=kLoop, calls=%fused_computation.102 | loop fusion | bytes 327680 | tf_op jit(solution)/shard_map/slice | solution.py:150
  119.3 11.9 %slice.406 = f32[5,65536]{0,1:T(8,128)S(1)} slice(f32[5,82944]{0,1:T(8,128)} %scatter_custom_fusion), slice={[0:5], [0:65536]} | slice | bytes 2621440 | tf_op jit(solution)/shard_map/slice | solution.py:147
  131.2 11.1 %copy-done = f32[5,65536]{0,1:T(8,128)} copy-done((f32[5,65536]{0,1:T(8,128)}, f32[5,65536]{0,1:T(8,128)S(1)}, u32[]{:S(2)}) %copy-start) | copy-done | bytes 1310744
  142.4 19.5 %copy.30 = f32[5,16,16,256]{3,2,1,0:T(8,128)S(1)} copy(f32[5,16,16,256]{0,3,2,1:T(8,128)} %bitcast.101) | data formatting | bytes 2621440 | tf_op jit(solution)/shard_map/reshape | solution.py:147
  162.0 2.8 %copy.33 = f32[5,16,256]{2,1,0:T(8,128)} copy(f32[5,16,256]{0,2,1:T(8,128)} %bitcast.103) | data formatting | bytes 163840 | tf_op jit(solution)/shard_map/reshape | solution.py:150
  164.8 2.2 copy.35
  178.8 2.9 %collective-permute-start.2 = (f32[1,24576]{1,0:T(1,128)S(1)}, f32[1,24576]{1,0:T(1,128)S(1)}, u32[]{:S(2)}, u32[]{:S(2)}) collective-permute-start(f32[1,24576]{1,0:T(1,128)S(1)} %get-tuple-element.129), channel_id=1, source_target_pairs={{0,1},{1,2},{2,3},{3,4},{4,5},{5,6},{6,7},{7,8},{8,9},{9,10},{10,1... | collective-permute-start | bytes 294920 | tf_op jit(solution)/shard_map/ppermute | solution.py:26
  185.0 3.2 %scatter-add.54 = f32[5,16,16,256]{3,2,1,0:T(8,128)S(1)} dynamic-update-slice(f32[5,16,16,256]{3,2,1,0:T(8,128)S(1)} %fusion.24, f32[5,16,1,256]{3,2,1,0:T(1,128)S(1)} %slice_add_fusion.2, s32[]{:T(128)} %constant.251.clone.1, s32[]{:T(128)} %constant.251.clone.1, s32[]{:T(128)} %constant.251.clone.1, s32[]{:T(128)} %constant.251.clone.1) | dynamic-update-slice | bytes 163844 | tf_op jit(solution)/shard_map/scatter-add | solution.py:178
  188.3 3.2 %scatter-add.55 = f32[5,16,16,256]{3,2,1,0:T(8,128)S(1)} dynamic-update-slice(f32[5,16,16,256]{3,2,1,0:T(8,128)S(1)} %scatter-add.54, f32[5,16,1,256]{3,2,1,0:T(1,128)S(1)} %slice_add_fusion.1, s32[]{:T(128)} %constant.251.clone.1, s32[]{:T(128)} %constant.251.clone.1, s32[]{:T(128)} %constant.277.clone.1, s32[]{:T(128)} %constant.251.clone.1) | dynamic-update-slice | bytes 163844 | tf_op jit(solution)/shard_map/scatter-add | solution.py:179
  193.7 5.1 %collective-permute-start.5 = (f32[1,16,256]{2,1,0:T(8,128)S(1)}, f32[1,16,256]{2,1,0:T(8,128)S(1)}, u32[]{:S(2)}, u32[]{:S(2)}) collective-permute-start(f32[1,16,256]{2,1,0:T(8,128)S(1)} %get-tuple-element.124), channel_id=1, source_target_pairs={{0,32},{32,64},{64,96},{96,128},{128,160},{160,192},{192,224},{1,3... | collective-permute-start | bytes 49160 | tf_op jit(solution)/shard_map/ppermute | solution.py:43
  200.1 4.0 %collective-permute-start.7 = (f32[16,1,256]{2,1,0:T(1,128)S(1)}, f32[16,1,256]{2,1,0:T(1,128)S(1)}, u32[]{:S(2)}, u32[]{:S(2)}) collective-permute-start(f32[16,1,256]{2,1,0:T(1,128)S(1)} %get-tuple-element.123), channel_id=1, source_target_pairs={{0,1},{1,2},{2,3},{3,4},{4,5},{5,6},{6,7},{7,8},{8,9},{9,10},{10,1... | collective-permute-start | bytes 49160 | tf_op jit(solution)/shard_map/ppermute | solution.py:43
  206.4 2.4 abs_reduce_fusion
  209.5 9.3 %pmax.35 = f32[]{:T(128)} all-reduce(f32[]{:T(128)} %add_reduce_fusion), channel_id=1, replica_groups=mesh['gx_0'=4,'gx_1'=2,'gy_0'=2,'gy_1'=4,'gy_2'=4] {'gx_0'}, use_global_device_ids=true, to_apply=%region_8.9 | all-reduce | flops 1 | bytes 8 | tf_op jit(solution)/shard_map/pmax | solution.py:57
  219.4 6.5 %pmax.36 = f32[]{:T(128)} all-reduce(f32[]{:T(128)} %pmax.35), channel_id=1, replica_groups=mesh['gx_0'=4,'gx_1'=2,'gy_0'=2,'gy_1'=4,'gy_2'=4] {'gx_1'}, use_global_device_ids=true, to_apply=%region_9.10 | all-reduce | flops 1 | bytes 8 | tf_op jit(solution)/shard_map/pmax | solution.py:57
  225.9 32.2 %pmax.37 = f32[]{:T(128)} all-reduce(f32[]{:T(128)} %pmax.36), channel_id=1, replica_groups=mesh['gx_0'=4,'gx_1'=2,'gy_0'=2,'gy_1'=4,'gy_2'=4] {'gy_0'}, use_global_device_ids=true, to_apply=%region_10.11 | all-reduce | flops 1 | bytes 8 | tf_op jit(solution)/shard_map/pmax | solution.py:57
  258.7 6.6 %pmax.38 = f32[]{:T(128)} all-reduce(f32[]{:T(128)} %pmax.37), channel_id=1, replica_groups=mesh['gx_0'=4,'gx_1'=2,'gy_0'=2,'gy_1'=4,'gy_2'=4] {'gy_1'}, use_global_device_ids=true, to_apply=%region_11.12 | all-reduce | flops 1 | bytes 8 | tf_op jit(solution)/shard_map/pmax | solution.py:57
  267.0 7.3 %pmax.39 = f32[]{:T(128)} all-reduce(f32[]{:T(128)} %pmax.38), channel_id=1, replica_groups=mesh['gx_0'=4,'gx_1'=2,'gy_0'=2,'gy_1'=4,'gy_2'=4] {'gy_2'}, use_global_device_ids=true, to_apply=%region_12.13 | all-reduce | flops 1 | bytes 8 | tf_op jit(solution)/shard_map/pmax | solution.py:57
  (96 shorter events, 39.1 us)
Async XLA Ops:
  12.3 22.5 %copy-start.4 = (f32[8192]{0:T(1024)S(1)}, f32[8192]{0:T(1024)}, u32[]{:S(2)}) copy-start(f32[8192]{0:T(1024)} %param.29) | copy-start | bytes 98308
  105.0 9.0 %copy-start.2 = (f32[3,8192]{1,0:T(4,128)S(1)}, f32[3,8192]{1,0:T(4,128)}, u32[]{:S(2)}) copy-start(f32[3,8192]{1,0:T(4,128)} %param.28) | copy-start | bytes 294916
  107.0 63.5 %collective-permute-start = (f32[1,27136]{1,0:T(1,128)}, f32[1,27136]{1,0:T(1,128)}, u32[]{:S(2)}, u32[]{:S(2)}) collective-permute-start(f32[1,27136]{1,0:T(1,128)} %get-tuple-element.127), channel_id=1, source_target_pairs={{0,32},{32,64},{64,96},{96,128},{128,160},{160,192},{192,224},{1,3... | collective-permute-start | bytes 325640 | tf_op jit(solution)/shard_map/ppermute | solution.py:26
  111.9 62.1 %collective-permute-start.1 = (f32[1,27136]{1,0:T(1,128)}, f32[1,27136]{1,0:T(1,128)}, u32[]{:S(2)}, u32[]{:S(2)}) collective-permute-start(f32[1,27136]{1,0:T(1,128)} %get-tuple-element.126), channel_id=1, source_target_pairs={{32,0},{64,32},{96,64},{128,96},{160,128},{192,160},{224,192},{33,... | collective-permute-start | bytes 325640 | tf_op jit(solution)/shard_map/ppermute | solution.py:28
  131.2 11.1 %copy-start = (f32[5,65536]{0,1:T(8,128)}, f32[5,65536]{0,1:T(8,128)S(1)}, u32[]{:S(2)}) copy-start(f32[5,65536]{0,1:T(8,128)S(1)} %slice.406) | copy-start | bytes 3932164
  170.5 21.1 %copy-start.5 = (f32[16,16,256]{2,1,0:T(8,128)S(1)}, f32[16,16,256]{2,1,0:T(8,128)}, u32[]{:S(2)}) copy-start(f32[16,16,256]{2,1,0:T(8,128)} %param.26) | copy-start | bytes 786436
  170.5 21.1 %copy-start.6 = (f32[16,16,256]{2,1,0:T(8,128)S(1)}, f32[16,16,256]{2,1,0:T(8,128)}, u32[]{:S(2)}) copy-start(f32[16,16,256]{2,1,0:T(8,128)} %param.24) | copy-start | bytes 786436
  178.8 6.0 %collective-permute-start.2 = (f32[1,24576]{1,0:T(1,128)S(1)}, f32[1,24576]{1,0:T(1,128)S(1)}, u32[]{:S(2)}, u32[]{:S(2)}) collective-permute-start(f32[1,24576]{1,0:T(1,128)S(1)} %get-tuple-element.129), channel_id=1, source_target_pairs={{0,1},{1,2},{2,3},{3,4},{4,5},{5,6},{6,7},{7,8},{8,9},{9,10},{10,1... | collective-permute-start | bytes 294920 | tf_op jit(solution)/shard_map/ppermute | solution.py:26
  182.7 5.5 %collective-permute-start.3 = (f32[1,24576]{1,0:T(1,128)S(1)}, f32[1,24576]{1,0:T(1,128)S(1)}, u32[]{:S(2)}, u32[]{:S(2)}) collective-permute-start(f32[1,24576]{1,0:T(1,128)S(1)} %get-tuple-element.128), channel_id=1, source_target_pairs={{1,0},{2,1},{3,2},{4,3},{5,4},{6,5},{7,6},{8,7},{9,8},{10,9},{11,1... | collective-permute-start | bytes 294920 | tf_op jit(solution)/shard_map/ppermute | solution.py:28
  191.7 17.1 %copy-start.1 = (f32[16,16,256]{2,1,0:T(8,128)}, f32[16,16,256]{2,1,0:T(8,128)S(1)}, u32[]{:S(2)}) copy-start(f32[16,16,256]{2,1,0:T(8,128)S(1)} %get-tuple-element.114) | copy-start | bytes 786436
  191.7 17.1 %copy-start.3 = (f32[16,16,256]{2,1,0:T(8,128)}, f32[16,16,256]{2,1,0:T(8,128)S(1)}, u32[]{:S(2)}) copy-start(f32[16,16,256]{2,1,0:T(8,128)S(1)} %get-tuple-element.107) | copy-start | bytes 786436
  191.8 14.4 %collective-permute-start.4 = (f32[1,16,256]{2,1,0:T(8,128)S(1)}, f32[1,16,256]{2,1,0:T(8,128)S(1)}, u32[]{:S(2)}, u32[]{:S(2)}) collective-permute-start(f32[1,16,256]{2,1,0:T(8,128)S(1)} %get-tuple-element.125), channel_id=1, source_target_pairs={{32,0},{64,32},{96,64},{128,96},{160,128},{192,160},{224,192},{33,... | collective-permute-start | bytes 49160 | tf_op jit(solution)/shard_map/ppermute | solution.py:44
  193.7 12.5 %collective-permute-start.5 = (f32[1,16,256]{2,1,0:T(8,128)S(1)}, f32[1,16,256]{2,1,0:T(8,128)S(1)}, u32[]{:S(2)}, u32[]{:S(2)}) collective-permute-start(f32[1,16,256]{2,1,0:T(8,128)S(1)} %get-tuple-element.124), channel_id=1, source_target_pairs={{0,32},{32,64},{64,96},{96,128},{128,160},{160,192},{192,224},{1,3... | collective-permute-start | bytes 49160 | tf_op jit(solution)/shard_map/ppermute | solution.py:43
  198.8 7.4 %collective-permute-start.6 = (f32[16,1,256]{2,1,0:T(1,128)S(1)}, f32[16,1,256]{2,1,0:T(1,128)S(1)}, u32[]{:S(2)}, u32[]{:S(2)}) collective-permute-start(f32[16,1,256]{2,1,0:T(1,128)S(1)} %get-tuple-element.122), channel_id=1, source_target_pairs={{1,0},{2,1},{3,2},{4,3},{5,4},{6,5},{7,6},{8,7},{9,8},{10,9},{11,1... | collective-permute-start | bytes 49160 | tf_op jit(solution)/shard_map/ppermute | solution.py:44
  200.1 6.1 %collective-permute-start.7 = (f32[16,1,256]{2,1,0:T(1,128)S(1)}, f32[16,1,256]{2,1,0:T(1,128)S(1)}, u32[]{:S(2)}, u32[]{:S(2)}) collective-permute-start(f32[16,1,256]{2,1,0:T(1,128)S(1)} %get-tuple-element.123), channel_id=1, source_target_pairs={{0,1},{1,2},{2,3},{3,4},{4,5},{5,6},{6,7},{7,8},{8,9},{9,10},{10,1... | collective-permute-start | bytes 49160 | tf_op jit(solution)/shard_map/ppermute | solution.py:43
where the time goes:
time: 281 us; the launch traced here: 276 us
  local copies, waits for them, and re-layouts  110 us (39%)
  other arithmetic  77.4 us (28%)
  blocking collectives  61.9 us (22%)
  starting transfers between devices  23.5 us (8%)
  between operations  3.61 us (1%)
    pmax x5, blocking collectives, over_axes(): shard = lax.pmax(shard, axis)  61.9 us
    scatter-add x1, other arithmetic, deposit_one(): return jax.ops.segment_sum(values, cell_slot, num_segments=total_cells)  61 us
    scatter x1, local copies, waits for them, and re-layouts, on_device(): buckets = jnp.zeros((9, 4 * capacity), jnp.float32).at[:, target].set(car...  21.1 us
    reshape x1, local copies, waits for them, and re-layouts, on_device(): core = flat_sums[:, :block_cells].reshape(5, cells_x, cells_y, depth_cells)  19.5 us
    unnamed x28, local copies, waits for them, and re-layouts  16.8 us
    slice x1, local copies, waits for them, and re-layouts, on_device(): core = flat_sums[:, :block_cells].reshape(5, cells_x, cells_y, depth_cells)  11.9 us
    ppermute x2, starting transfers between devices, padded_2(): lax.ppermute(last, axis, up)  9.06 us
    ppermute x2, starting transfers between devices, with_halo(): lax.ppermute(tail, axis, [(i, (i + 1) % count) for i in range(ends)])  7.86 us
  transfers between devices with their start and end apart: 8, of which 0 were waited for; matrix products, arithmetic and copies ran while one was open for 20% of the time, Pallas kernels for 0%

commit v1 on v0

v1 whole, which is shorter than its diff:
```python
import functools

import jax
import jax.numpy as jnp
from jax import lax
from jax.experimental import pallas as pl
from jax.experimental.pallas import tpu as pltpu
from jax.sharding import PartitionSpec as P

ADIABATIC_INDEX = 1.4
KICK = 0.25
COURANT = 0.4
SHRINK = 0.5
FACES = 4
F32 = jnp.float32
BF16 = jnp.bfloat16
MESH = pl.DeviceIdType.MESH
VMEM = pltpu.VMEM
ANY = pl.ANY


def row_iota(shape):
    return lax.broadcasted_iota(jnp.int32, shape, 0)


def lane_iota(shape):
    return lax.broadcasted_iota(jnp.int32, shape, 1)


def pack_left(cells, shift, steps):
    width = cells.shape[1]
    for k in range(steps):
        step = 1 << k
        coming = pltpu.roll(cells, width - step, axis=1)
        coming_shift = pltpu.roll(shift, width - step, axis=1)
        take = (coming_shift & step) != 0
        leave = (shift & step) != 0
        cells = jnp.where(take, coming, cells)
        shift = jnp.where(take, coming_shift, jnp.where(leave, 0, shift))
    return cells, shift


def sort_kernel(cells_x, cells_y, mass, vel, temp, cell, count, stay_out, bucket_out):
    rows = mass.shape[1]
    move = rows // 16
    chunk = 256
    chunks = rows // chunk
    anchor_x = lax.axis_index("gx") * cells_x
    anchor_y = lax.axis_index("gy") * cells_y
    live = lane_iota((1, rows)) < count[0]
    m, t = mass[...], temp[...]
    boiled = m * (1.0 / (1.0 + jnp.exp(4.0 - 2.0 * t)))
    left = m - SHRINK * boiled
    local_x = cell[0:1, :] - anchor_x
    local_y = cell[1:2, :] - anchor_y
    heading = jnp.where(
        local_x < 0,
        0,
        jnp.where(
            local_x >= cells_x, 1, jnp.where(local_y < 0, 2, jnp.where(local_y >= cells_y, 3, 4))
        ),
    )
    heading = jnp.where(live, heading, 5)
    record = jnp.concatenate([left, vel[...], t, cell[...].astype(F32)], axis=0)
    heads = jnp.broadcast_to(heading, (8, rows))
    stay_out[...] = jnp.where(heads == 4, record, 0.0)

    sub = row_iota((8, rows))
    mask = jnp.where((sub == heads) & (sub < 4), 1.0, 0.0)
    mask = jnp.where((sub == 4) & (heads < 4), 1.0, mask)
    stacked = jnp.concatenate(
        [mask[:, c * chunk : (c + 1) * chunk] for c in range(chunks)], axis=0
    ).astype(BF16)
    a, b = row_iota((chunk, chunk)), lane_iota((chunk, chunk))
    upper = jnp.where(a < b, 1.0, 0.0).astype(BF16)
    inside = jnp.dot(stacked, upper, preferred_element_type=F32)
    total = jnp.dot(stacked, jnp.ones((chunk, chunk), BF16), preferred_element_type=F32)
    n = 8 * chunks
    a, b = row_iota((n, n)), lane_iota((n, n))
    ahead = jnp.where(((a & 7) == (b & 7)) & (b < a), 1.0, 0.0).astype(BF16)
    before = jnp.dot(ahead, total.astype(BF16), preferred_element_type=F32)
    ranks = inside + before
    rank = jnp.concatenate([ranks[c * 8 : (c + 1) * 8] for c in range(chunks)], axis=1)
    counts = (before + total)[n - 8 : n, :128].astype(jnp.int32)

    own = jnp.sum(jnp.where(sub < 4, mask * rank, 0.0), axis=0, keepdims=True).astype(jnp.int32)
    overall = rank[4:5].astype(jnp.int32)
    moves = heading < 4
    shift = lane_iota((1, rows)) - overall
    target = heading * move + own
    shift = jnp.where(moves, shift + target * rows, 0)
    packed, key = pack_left(record, jnp.broadcast_to(shift, (8, rows)), rows.bit_length() - 1)

    wide = FACES * move
    packed = packed[:, :wide]
    slot = key[:, :wide] // rows
    place = lane_iota((8, wide))
    present = place < jnp.concatenate([counts[4:5]] * (wide // 128), axis=1)
    for h in range(FACES):
        mine = present & (slot // move == h)
        gap = jnp.where(mine, place - (slot - h * move), 0)
        out, _ = pack_left(packed, gap, wide.bit_length() - 1)
        full = jnp.concatenate([counts[h : h + 1]] * (move // 128), axis=1)
        bucket_out[h] = jnp.where(lane_iota((8, move)) < full, out[:, :move], 0.0)


def main_kernel(
    nx,
    ny,
    cells_x,
    cells_y,
    stay,
    bucket,
    density,
    momentum,
    energy,
    density_out,
    momentum_out,
    energy_out,
    arrived_out,
    step_out,
    dens,
    mom,
    ener,
    press,
    dep,
    got,
    side,
    halo,
    best,
    best_in,
    load_sem,
    store_sem,
    bucket_send,
    bucket_recv,
    halo_send,
    halo_recv,
    best_send,
    best_recv,
):
    i, j = lax.axis_index("gx"), lax.axis_index("gy")
    cols = cells_x * cells_y
    depth = press.shape[1]
    rows = stay.shape[1]
    move = got.shape[2]
    up_x, down_x = lax.rem(i + 1, nx), lax.rem(i + nx - 1, nx)
    up_y, down_y = lax.rem(j + 1, ny), lax.rem(j + ny - 1, ny)
    near = [(down_x, j), (up_x, j), (i, down_y), (i, up_y)]
    half = ny // 2
    spot = lax.div(j, half) * nx + i
    lane = lax.rem(j, half)
    size_a, size_b = 2 * nx, half
    first = []
    for q in range(1, size_a):
        there = lax.rem(spot + q, size_a)
        first.append((lax.rem(there, nx), lax.div(there, nx) * half + lane))
    second = []
    for q in range(1, size_b):
        second.append((i, lax.div(j, half) * half + lax.rem(lane + q, size_b)))

    barrier = pltpu.get_barrier_semaphore()
    everyone = near + first + second
    for peer in everyone:
        pl.semaphore_signal(barrier, inc=1, device_id=peer, device_id_type=MESH)

    loads = [
        pltpu.make_async_copy(energy, ener, load_sem.at[0]),
        pltpu.make_async_copy(density, dens, load_sem.at[1]),
        pltpu.make_async_copy(momentum, mom, load_sem.at[2]),
    ]
    for load in loads:
        load.start()

    anchor_x, anchor_y = i * cells_x, j * cells_y

    def terms(table, fields):
        v = table[1:4]
        t = table[4:5]
        boiled = table[0:1] / (0.5 + jnp.exp(4.0 - 2.0 * t))
        parts = []
        for f in fields:
            if f == 0:
                s = boiled
            elif f < 4:
                s = boiled * v[f - 1 : f]
            else:
                s = boiled * (t + 0.5 * jnp.sum(v * v, axis=0, keepdims=True))
            high = s.astype(BF16)
            low = (s - high.astype(F32)).astype(BF16)
            parts.append((high, low))
        width = table.shape[1]
        local = table[5:6].astype(jnp.int32) - anchor_x
        local = local * cells_y + table[6:7].astype(jnp.int32) - anchor_y
        column = jnp.where((local >= 0) & (local < cols), local, -1).astype(F32).astype(BF16)
        deep = table[7:8].astype(BF16)
        return parts, column, deep

    def deposit(table, fields):
        parts, column, deep = terms(table, fields)
        width = table.shape[1]
        which = row_iota((cols, width)).astype(F32).astype(BF16)
        there = which == column
        layer = row_iota((depth, width)).astype(F32).astype(BF16)
        pick = jnp.where(layer == deep, BF16(1), BF16(0))
        for f, halves in zip(fields, parts):
            both = jnp.concatenate([jnp.where(there, s, BF16(0)) for s in halves], axis=0)
            sums = lax.dot_general(
                both, pick, (((1,), (1,)), ((), ())), preferred_element_type=F32
            )
            dep[f] += sums[:cols] + sums[cols:]

    wide = 2 * move

    def deposit_stay(fields):
        def body(c, carry):
            deposit(stay[:, pl.ds(pl.multiple_of(c * wide, wide), wide)], fields)
            return carry

        lax.fori_loop(0, rows // wide, body, 0)

    def deposit_got(fields):
        for c in range(2):
            deposit(jnp.concatenate([got[2 * c], got[2 * c + 1]], axis=1), fields)

    dep[...] = jnp.zeros_like(dep)
    deposit_stay((4,))

    pl.semaphore_wait(barrier, len(everyone))
    sends = []
    for h in range(FACES):
        sends.append(
            pltpu.make_async_remote_copy(
                src_ref=bucket.at[h],
                dst_ref=got.at[h ^ 1],
                send_sem=bucket_send.at[h],
                recv_sem=bucket_recv.at[h ^ 1],
                device_id=near[h],
                device_id_type=MESH,
            )
        )
    for send in sends:
        send.start()
    deposit_stay((0, 1))
    for send in sends:
        send.wait()
    deposit_got((4,))
    loads[0].wait()
    total = ener[...] + dep[4]
    ener[...] = total
    press[...] = (ADIABATIC_INDEX - 1.0) * total
    for x in range(cells_x):
        side[0, pl.ds(x, 1)] = press[pl.ds(x * cells_y, 1)]
        side[1, pl.ds(x, 1)] = press[pl.ds(x * cells_y + cells_y - 1, 1)]
    outs = [
        pltpu.make_async_copy(ener, energy_out, store_sem.at[0]),
        pltpu.make_async_copy(got, arrived_out, store_sem.at[1]),
    ]
    for out in outs:
        out.start()
    faces = [
        press.at[pl.ds(0, cells_y)],
        press.at[pl.ds(cols - cells_y, cells_y)],
        side.at[0],
        side.at[1],
    ]
    sides = []
    for h in range(FACES):
        sides.append(
            pltpu.make_async_remote_copy(
                src_ref=faces[h],
                dst_ref=halo.at[h ^ 1],
                send_sem=halo_send.at[h],
                recv_sem=halo_recv.at[h ^ 1],
                device_id=near[h],
                device_id_type=MESH,
            )
        )
    for send in sides:
        send.start()
    deposit_got((0, 1, 2, 3))
    deposit_stay((2, 3))
    for load in loads[1:]:
        load.wait()
    for send in sides:
        send.wait()

    low_x = jnp.where(i > 0, halo[0], 0.0)
    high_x = jnp.where(i < nx - 1, halo[1], 0.0)
    low_y = jnp.where(j > 0, halo[2], 0.0)
    high_y = jnp.where(j < ny - 1, halo[3], 0.0)
    z = lane_iota((cells_y, depth))
    y = row_iota((cells_y, depth))
    fastest = jnp.zeros((cells_y, depth), F32)
    for x in range(cells_x):
        here = pl.ds(x * cells_y, cells_y)
        p = press[here]
        before = press[pl.ds((x - 1) * cells_y, cells_y)] if x else low_x
        after = press[pl.ds((x + 1) * cells_y, cells_y)] if x < cells_x - 1 else high_x
        below = jnp.where(y == 0, low_y[x : x + 1], pltpu.roll(p, 1, axis=0))
        above = jnp.where(y == cells_y - 1, high_y[x : x + 1], pltpu.roll(p, cells_y - 1, axis=0))
        under = jnp.where(z == 0, 0.0, pltpu.roll(p, 1, axis=1))
        over = jnp.where(z == depth - 1, 0.0, pltpu.roll(p, depth - 1, axis=1))
        rho = dens[here] + dep[0, here]
        dens[here] = rho
        wave = jnp.zeros_like(p)
        for k, (a, b) in enumerate(((before, after), (below, above), (under, over))):
            impulse = mom[k, here] + dep[k + 1, here] - KICK * (0.5 * (b - a))
            mom[k, here] = impulse
            wave = jnp.maximum(wave, jnp.abs(impulse / rho))
        wave = wave + jnp.sqrt(ADIABATIC_INDEX * p / rho)
        fastest = jnp.maximum(fastest, wave)
    late = [
        pltpu.make_async_copy(mom, momentum_out, store_sem.at[2]),
        pltpu.make_async_copy(dens, density_out, store_sem.at[3]),
    ]
    for out in late:
        out.start()
    top = jnp.max(fastest, axis=0, keepdims=True)
    top = jnp.maximum(top[:, :128], top[:, 128:])
    for phase, peers in enumerate((first, second)):
        best[phase] = top
        copies = []
        for q, peer in enumerate(peers):
            copies.append(
                pltpu.make_async_remote_copy(
                    src_ref=best.at[phase],
                    dst_ref=best_in.at[phase, q],
                    send_sem=best_send.at[phase, q],
                    recv_sem=best_recv.at[phase, q],
                    device_id=peer,
                    device_id_type=MESH,
                )
            )
        for copy in copies:
            copy.start()
        for copy in copies:
            copy.wait()
        for q in range(len(peers)):
            top = jnp.maximum(top, best_in[phase, q])
    step_out[...] = COURANT / jnp.broadcast_to(jnp.max(top, axis=1, keepdims=True), (1, 128))
    for out in outs + late:
        out.wait()


def on_device(density, momentum, energy, mass, velocity, temp, cell, count):
    cells_x, cells_y, depth = density.shape
    rows = mass.shape[0]
    move = rows // 16
    cols = cells_x * cells_y
    vmem = pl.BlockSpec(memory_space=VMEM)
    anyspace = pl.BlockSpec(memory_space=ANY)
    stay, bucket = pl.pallas_call(
        functools.partial(sort_kernel, cells_x, cells_y),
        name="sort_parcels",
        out_shape=(
            jax.ShapeDtypeStruct((8, rows), F32),
            jax.ShapeDtypeStruct((FACES, 8, move), F32),
        ),
        in_specs=[vmem] * 4 + [pl.BlockSpec(memory_space=pltpu.SMEM)],
        out_specs=(vmem, vmem),
        compiler_params=pltpu.CompilerParams(vmem_limit_bytes=48 * 2**20),
    )(mass.reshape(1, rows), velocity, temp.reshape(1, rows), cell, count)
    nx, ny = lax.axis_size("gx"), lax.axis_size("gy")
    field = jax.ShapeDtypeStruct((cols, depth), F32)
    dens, mom, ener, arrived, step = pl.pallas_call(
        functools.partial(main_kernel, nx, ny, cells_x, cells_y),
        name="deposit_and_push",
        out_shape=(
            field,
            jax.ShapeDtypeStruct((3, cols, depth), F32),
            field,
            jax.ShapeDtypeStruct((FACES, 8, move), F32),
            jax.ShapeDtypeStruct((1, 128), F32),
        ),
        in_specs=[vmem, vmem, anyspace, anyspace, anyspace],
        out_specs=(anyspace, anyspace, anyspace, anyspace, vmem),
        scratch_shapes=[
            VMEM((cols, depth), F32),
            VMEM((3, cols, depth), F32),
            VMEM((cols, depth), F32),
            VMEM((cols, depth), F32),
            VMEM((5, cols, depth), F32),
            VMEM((FACES, 8, move), F32),
            VMEM((2, cells_x, depth), F32),
            VMEM((FACES, cells_y, depth), F32),
            VMEM((2, 1, 128), F32),
            VMEM((2, 15, 1, 128), F32),
            pltpu.SemaphoreType.DMA((3,)),
            pltpu.SemaphoreType.DMA((4,)),
            pltpu.SemaphoreType.DMA((FACES,)),
            pltpu.SemaphoreType.DMA((FACES,)),
            pltpu.SemaphoreType.DMA((FACES,)),
            pltpu.SemaphoreType.DMA((FACES,)),
            pltpu.SemaphoreType.DMA((2, 15)),
            pltpu.SemaphoreType.DMA((2, 15)),
        ],
        compiler_params=pltpu.CompilerParams(
            vmem_limit_bytes=56 * 2**20, collective_id=0, has_side_effects=True
        ),
    )(
        stay,
        bucket,
        density.reshape(cols, depth),
        momentum.reshape(3, cols, depth),
        energy.reshape(cols, depth),
    )
    table = jnp.concatenate([stay] + [arrived[h] for h in range(FACES)], axis=1)
    return (
        dens.reshape(density.shape),
        mom.reshape(momentum.shape),
        ener.reshape(energy.shape),
        table[:5],
        table[5:].astype(jnp.int32),
        step[0, 0],
    )


def solution(mesh):
    both = ("gx", "gy")
    return jax.shard_map(
        on_device,
        mesh=mesh,
        in_specs=(
            P("gx", "gy", None),
            P(None, "gx", "gy", None),
            P("gx", "gy", None),
            P(both),
            P(None, both),
            P(both),
            P(None, both),
            P(both),
        ),
        out_specs=(
            P("gx", "gy", None),
            P(None, "gx", "gy", None),
            P("gx", "gy", None),
            P(None, both),
            P(None, both),
            P(),
        ),
        check_vma=False,
    )
```

time: 281 us -> 59.2 us (0.21); the launches traced: 276 us -> 58.7 us
  local copies, waits for them, and re-layouts: 110 us -> 11.1 us
  other arithmetic: 77.4 us -> 0.77 us
  blocking collectives: 61.9 us -> 0 us
  Pallas kernels: 0 us -> 44.3 us
  starting transfers between devices: 23.5 us -> 0 us
    scatter-add x3 -> x0, other arithmetic: 61.9 us -> none  [the longest x1 61 us: deposit_one(): return jax.ops.segment_sum(values, cell_slot, num_segments=total_cells)]
    pmax x5 -> x0, blocking collectives: 61.9 us -> none  [over_axes(): shard = lax.pmax(shard, axis)]
    pallas_call x0 -> x2, Pallas kernels: none -> 44.3 us  [the longest x1 40.6 us: on_device(): pl.pallas_call(functools.partial(main_kernel, nx, ny, cells_x, cells_y),...]
    slice x17 -> x0, local copies, waits for them, and re-layouts: 29.3 us -> none  [the longest x1 11.9 us: on_device(): core = flat_sums[:, :block_cells].reshape(5, cells_x, cells_y, depth_cells)]
    reshape x3 -> x0, local copies, waits for them, and re-layouts: 24.6 us -> none  [the longest x1 19.5 us: on_device(): core = flat_sums[:, :block_cells].reshape(5, cells_x, cells_y, depth_cells)]
    ppermute x8 -> x0, starting transfers between devices: 23.5 us -> none  [the longest x2 9.06 us: padded_2(): lax.ppermute(last, axis, up)]
    scatter x1 -> x0, local copies, waits for them, and re-layouts: 21.1 us -> none  [on_device(): buckets = jnp.zeros((9, 4 * capacity), jnp.float32).at[:, target].set(car...]
    scatter-add x6 -> x0, local copies, waits for them, and re-layouts: 9.38 us -> none  [the longest x1 3.23 us: on_device(): core.at[:, :, 0].add(got_y[0, :size_y].reshape(5, cells_x, depth_cells))]
  transfers between devices with their start and end apart: 8 -> 0, of which waited for: 0 -> 0; matrix products, arithmetic and copies ran while one was open for 20% -> 0% of each run, Pallas kernels for 0% -> 0%
where the time goes in v1:
time: 59.2 us; the launch traced here: 58.7 us
  Pallas kernels  44.3 us (75%)
  local copies, waits for them, and re-layouts  11.1 us (19%)
  between operations  2.5 us (4%)
  other arithmetic  0.77 us (1%)
    pallas_call x1, Pallas kernels, on_device(): pl.pallas_call(functools.partial(main_kernel, nx, ny, cells_x, cells_y),...  40.6 us
    unnamed x27, local copies, waits for them, and re-layouts  10.3 us
    pallas_call x1, Pallas kernels, on_device(): pl.pallas_call(functools.partial(sort_kernel, cells_x, cells_y), name='so...  3.77 us

profile of v1, /device:TPU:1, one launch (start us, length us, event | category | flops | bytes accessed | tf_op | source)
XLA Modules:
  0.0 58.7 jit_solution(12214426379311221508)
XLA Ops:
  1.3 0.0 copy-start.1
  1.3 0.9 %copy-done.1 = f32[3,8192]{1,0:T(4,128)S(1)} copy-done((f32[3,8192]{1,0:T(4,128)S(1)}, f32[3,8192]{1,0:T(4,128)}, u32[]{:S(2)}) %copy-start.1) | copy-done | bytes 98328
  2.2 0.0 copy-start.2
  2.2 0.9 %copy-done.2 = s32[3,8192]{1,0:T(4,128)S(1)} copy-done((s32[3,8192]{1,0:T(4,128)S(1)}, s32[3,8192]{1,0:T(4,128)}, u32[]{:S(2)}) %copy-start.2) | copy-done | bytes 98328
  3.1 0.8 %copy-done.4 = f32[8192]{0:T(1024)S(1)} copy-done((f32[8192]{0:T(1024)S(1)}, f32[8192]{0:T(1024)}, u32[]{:S(2)}) %copy-start.4) | copy-done | bytes 32792
  3.9 0.8 %copy-done.5 = f32[8192]{0:T(1024)S(1)} copy-done((f32[8192]{0:T(1024)S(1)}, f32[8192]{0:T(1024)}, u32[]{:S(2)}) %copy-start.5) | copy-done | bytes 32792
  4.6 3.8 %sort_parcels.1 = (f32[8,8192]{1,0:T(8,128)S(1)}, f32[4,8,512]{2,1,0:T(8,128)S(1)}) custom-call(f32[1,8192]{1,0:T(1,128)S(1)} %bitcast.19, f32[3,8192]{1,0:T(4,128)S(1)} %copy-done.1, f32[1,8192]{1,0:T(1,128)S(1)} %bitcast.20, s32[3,8192]{1,0:T(4,128)S(1)} %copy-done.2, s32[1]{0:T(128)S(6)} %copy.22.count), custom_call_target="tpu_custom_call" | custom-call | tf_op jit(solution)/shard_map/sort_parcels/pallas_call | solution.py:352
  8.4 0.0 copy-start.3
  8.4 0.6 %copy-done.3 = f32[4,8,512]{2,1,0:T(8,128)} copy-done((f32[4,8,512]{2,1,0:T(8,128)}, f32[4,8,512]{2,1,0:T(8,128)S(1)}, u32[]{:S(2)}) %copy-start.3) | copy-done | bytes 65560
  9.0 0.7 %copy-done = f32[8,8192]{1,0:T(8,128)} copy-done((f32[8,8192]{1,0:T(8,128)}, f32[8,8192]{1,0:T(8,128)S(1)}, u32[]{:S(2)}) %copy-start) | copy-done | bytes 262168
  9.7 40.6 %deposit_and_push.1 = (f32[256,256]{1,0:T(8,128)}, f32[3,256,256]{2,1,0:T(8,128)}, f32[256,256]{1,0:T(8,128)}, f32[4,8,512]{2,1,0:T(8,128)}, f32[1,128]{1,0:T(1,128)}) custom-call(f32[8,8192]{1,0:T(8,128)} %copy-done, f32[4,8,512]{2,1,0:T(8,128)} %copy-done.3, f32[256,256]{1,0:T(8,128)} %bitcast.24, f32[3,256,256]{2,1,0:T(8,128)} %bitcast.21, ...), custom_call_target="tpu_custom_call" | custom-call | tf_op jit(solution)/shard_map/deposit_and_push/pallas_call | solution.py:365
  50.3 0.0 copy-start.6
  50.3 0.8 %bitcast_dynamic-update-slice_fusion.3 = f32[8,10240]{1,0:T(8,128)S(1)} fusion(f32[8,10240]{1,0:T(8,128)S(1)} %constant_dynamic-update-slice_fusion, f32[4,8,512]{2,1,0:T(8,128)} %get-tuple-element.18), kind=kLoop, calls=%fused_computation.4 | loop fusion | bytes 32768
  51.1 0.7 %bitcast_dynamic-update-slice_fusion.2 = f32[8,10240]{1,0:T(8,128)S(1)} fusion(f32[8,10240]{1,0:T(8,128)S(1)} %bitcast_dynamic-update-slice_fusion.3, f32[4,8,512]{2,1,0:T(8,128)} %get-tuple-element.18), kind=kLoop, calls=%fused_computation.3 | loop fusion | bytes 32768
  51.8 0.7 %bitcast_dynamic-update-slice_fusion.1 = f32[8,10240]{1,0:T(8,128)S(1)} fusion(f32[8,10240]{1,0:T(8,128)S(1)} %bitcast_dynamic-update-slice_fusion.2, f32[4,8,512]{2,1,0:T(8,128)} %get-tuple-element.18), kind=kLoop, calls=%fused_computation.2 | loop fusion | bytes 32768
  52.5 0.7 %bitcast_dynamic-update-slice_fusion = f32[8,10240]{1,0:T(8,128)S(1)} fusion(f32[8,10240]{1,0:T(8,128)S(1)} %bitcast_dynamic-update-slice_fusion.1, f32[4,8,512]{2,1,0:T(8,128)} %get-tuple-element.18), kind=kLoop, calls=%fused_computation.1 | loop fusion | bytes 32768 | tf_op jit(solution)/shard_map/concatenate | solution.py:407
  53.3 0.8 %slice_convert_fusion = s32[3,10240]{1,0:T(4,128)} fusion(f32[8,10240]{1,0:T(8,128)S(1)} %bitcast_dynamic-update-slice_fusion), kind=kLoop, calls=%fused_computation | loop fusion | flops 30720 | bytes 245760 | tf_op jit(solution)/shard_map/convert_element_type | solution.py:413
  54.0 1.7 %copy.23 = f32[16,16,256]{2,1,0:T(8,128)} copy(f32[16,16,256]{2,1,0:T(8,128)} %bitcast.27) | data formatting | bytes 524288
  55.7 0.0 copy-done.7
  55.7 0.0 copy-done.6
  55.7 0.9 %copy.24 = f32[3,16,16,256]{3,2,1,0:T(8,128)} copy(f32[3,16,16,256]{3,2,1,0:T(8,128)S(1)} %bitcast.22) | data formatting | bytes 1572864
  56.6 0.2 copy-done.8
  56.8 0.7 %copy.25 = f32[16,16,256]{2,1,0:T(8,128)} copy(f32[16,16,256]{2,1,0:T(8,128)S(1)} %bitcast.26) | data formatting | bytes 524288
  57.5 0.0 copy-done.9
  (7 shorter events, 0.0 us)
Async XLA Ops:
  1.3 0.9 %copy-start.1 = (f32[3,8192]{1,0:T(4,128)S(1)}, f32[3,8192]{1,0:T(4,128)}, u32[]{:S(2)}) copy-start(f32[3,8192]{1,0:T(4,128)} %vel.1) | copy-start | bytes 294916
  2.2 0.9 %copy-start.2 = (s32[3,8192]{1,0:T(4,128)S(1)}, s32[3,8192]{1,0:T(4,128)}, u32[]{:S(2)}) copy-start(s32[3,8192]{1,0:T(4,128)} %cell.1) | copy-start | bytes 294916
  3.1 0.8 %copy-start.4 = (f32[8192]{0:T(1024)S(1)}, f32[8192]{0:T(1024)}, u32[]{:S(2)}) copy-start(f32[8192]{0:T(1024)} %param.11) | copy-start | bytes 98308
  3.8 0.8 %copy-start.5 = (f32[8192]{0:T(1024)S(1)}, f32[8192]{0:T(1024)}, u32[]{:S(2)}) copy-start(f32[8192]{0:T(1024)} %param.13) | copy-start | bytes 98308
  8.4 0.6 %copy-start.3 = (f32[4,8,512]{2,1,0:T(8,128)}, f32[4,8,512]{2,1,0:T(8,128)S(1)}, u32[]{:S(2)}) copy-start(f32[4,8,512]{2,1,0:T(8,128)S(1)} %get-tuple-element.14.bucket) | copy-start | bytes 196612
  9.0 0.7 %copy-start = (f32[8,8192]{1,0:T(8,128)}, f32[8,8192]{1,0:T(8,128)S(1)}, u32[]{:S(2)}) copy-start(f32[8,8192]{1,0:T(8,128)S(1)} %get-tuple-element.13.stay) | copy-start | bytes 786436
  50.3 5.4 %copy-start.6 = (f32[3,256,256]{2,1,0:T(8,128)S(1)}, f32[3,256,256]{2,1,0:T(8,128)}, u32[]{:S(2)}) copy-start(f32[3,256,256]{2,1,0:T(8,128)} %get-tuple-element.16) | copy-start | bytes 2359300
  53.3 2.4 %copy-start.7 = (f32[8,10240]{1,0:T(8,128)}, f32[8,10240]{1,0:T(8,128)S(1)}, u32[]{:S(2)}) copy-start(f32[8,10240]{1,0:T(8,128)S(1)} %bitcast_dynamic-update-slice_fusion) | copy-start | bytes 983044
  55.7 1.1 %copy-start.8 = (f32[256,256]{1,0:T(8,128)S(1)}, f32[256,256]{1,0:T(8,128)}, u32[]{:S(2)}) copy-start(f32[256,256]{1,0:T(8,128)} %get-tuple-element.17) | copy-start | bytes 786436
  56.8 0.7 %copy-start.9 = (f32[1,128]{1,0:T(1,128)S(1)}, f32[1,128]{1,0:T(1,128)}, u32[]{:S(2)}) copy-start(f32[1,128]{1,0:T(1,128)} %get-tuple-element.19) | copy-start | bytes 1540

commit v2 on v1

--- a/solution.py
+++ b/solution.py
@@ -16,7 +16,7 @@
 BF16 = jnp.bfloat16
 MESH = pl.DeviceIdType.MESH
 VMEM = pltpu.VMEM
-ANY = pl.ANY
+HBM = pltpu.HBM
 
 
 def row_iota(shape):
@@ -40,13 +40,13 @@
     return cells, shift
 
 
-def sort_kernel(cells_x, cells_y, mass, vel, temp, cell, count, stay_out, bucket_out):
+def sort_parcels(
+    cells_x, cells_y, anchor_x, anchor_y, mass, vel, temp, cell, count, stay_out, bucket_out
+):
     rows = mass.shape[1]
     move = rows // 16
     chunk = 256
     chunks = rows // chunk
-    anchor_x = lax.axis_index("gx") * cells_x
-    anchor_y = lax.axis_index("gy") * cells_y
     live = lane_iota((1, rows)) < count[0]
     m, t = mass[...], temp[...]
     boiled = m * (1.0 / (1.0 + jnp.exp(4.0 - 2.0 * t)))
@@ -104,33 +104,40 @@
         bucket_out[h] = jnp.where(lane_iota((8, move)) < full, out[:, :move], 0.0)
 
 
-def main_kernel(
+def fused_kernel(
     nx,
     ny,
     cells_x,
     cells_y,
-    stay,
-    bucket,
+    mass,
+    vel,
+    temp,
+    cell,
+    count,
     density,
     momentum,
     energy,
-    density_out,
-    momentum_out,
-    energy_out,
-    arrived_out,
-    step_out,
     dens,
     mom,
     ener,
+    state_out,
+    cell_out,
+    step_out,
+    mass_in,
+    vel_in,
+    temp_in,
+    cell_in,
+    stay,
+    bucket,
     press,
     dep,
+    rim,
     got,
     side,
     halo,
     best,
     best_in,
     load_sem,
-    store_sem,
     bucket_send,
     bucket_recv,
     halo_send,
@@ -163,15 +170,30 @@
     for peer in everyone:
         pl.semaphore_signal(barrier, inc=1, device_id=peer, device_id_type=MESH)
 
+    pairs = [
+        (cell, cell_in),
+        (mass, mass_in),
+        (temp, temp_in),
+        (vel, vel_in),
+        (energy, ener),
+        (density, dens),
+        (momentum, mom),
+    ]
     loads = [
-        pltpu.make_async_copy(energy, ener, load_sem.at[0]),
-        pltpu.make_async_copy(density, dens, load_sem.at[1]),
-        pltpu.make_async_copy(momentum, mom, load_sem.at[2]),
+        pltpu.make_async_copy(src, dst, load_sem.at[n]) for n, (src, dst) in enumerate(pairs)
     ]
     for load in loads:
         load.start()
+    dep[...] = jnp.zeros_like(dep)
+    for load in loads[:4]:
+        load.wait()
 
     anchor_x, anchor_y = i * cells_x, j * cells_y
+    sort_parcels(
+        cells_x, cells_y, anchor_x, anchor_y, mass_in, vel_in, temp_in, cell_in, count, stay, bucket
+    )
+    state_out[:, :rows] = stay[:5]
+    cell_out[:, :rows] = stay[5:].astype(jnp.int32)
 
     def terms(table, fields):
         v = table[1:4]
@@ -188,42 +210,53 @@
             high = s.astype(BF16)
             low = (s - high.astype(F32)).astype(BF16)
             parts.append((high, low))
-        width = table.shape[1]
-        local = table[5:6].astype(jnp.int32) - anchor_x
-        local = local * cells_y + table[6:7].astype(jnp.int32) - anchor_y
-        column = jnp.where((local >= 0) & (local < cols), local, -1).astype(F32).astype(BF16)
-        deep = table[7:8].astype(BF16)
-        return parts, column, deep
-
-    def deposit(table, fields):
-        parts, column, deep = terms(table, fields)
-        width = table.shape[1]
-        which = row_iota((cols, width)).astype(F32).astype(BF16)
-        there = which == column
-        layer = row_iota((depth, width)).astype(F32).astype(BF16)
-        pick = jnp.where(layer == deep, BF16(1), BF16(0))
-        for f, halves in zip(fields, parts):
-            both = jnp.concatenate([jnp.where(there, s, BF16(0)) for s in halves], axis=0)
-            sums = lax.dot_general(
-                both, pick, (((1,), (1,)), ((), ())), preferred_element_type=F32
-            )
-            dep[f] += sums[:cols] + sums[cols:]
+        return parts
+
+    def picked(index, size):
+        which = row_iota((size, index.shape[1])).astype(F32).astype(BF16)
+        return which == index.astype(F32).astype(BF16)
+
+    def sums_of(both, pick):
+        return lax.dot_general(both, pick, (((1,), (1,)), ((), ())), preferred_element_type=F32)
 
     wide = 2 * move
 
     def deposit_stay(fields):
         def body(c, carry):
-            deposit(stay[:, pl.ds(pl.multiple_of(c * wide, wide), wide)], fields)
+            table = stay[:, pl.ds(pl.multiple_of(c * wide, wide), wide)]
+            parts = terms(table, fields)
+            local_x = table[5:6].astype(jnp.int32) - anchor_x
+            local_y = table[6:7].astype(jnp.int32) - anchor_y
+            there = picked(local_x * cells_y + local_y, cols)
+            pick = jnp.where(picked(table[7:8], depth), BF16(1), BF16(0))
+            for f, halves in zip(fields, parts):
+                both = jnp.concatenate([jnp.where(there, s, BF16(0)) for s in halves], axis=0)
+                sums = sums_of(both, pick)
+                dep[f] += sums[:cols] + sums[cols:]
             return carry
 
         lax.fori_loop(0, rows // wide, body, 0)
 
-    def deposit_got(fields):
-        for c in range(2):
-            deposit(jnp.concatenate([got[2 * c], got[2 * c + 1]], axis=1), fields)
-
-    dep[...] = jnp.zeros_like(dep)
-    deposit_stay((4,))
+    def deposit_got():
+        for b in range(FACES):
+            table = got[b]
+            parts = terms(table, range(5))
+            if b < 2:
+                along, length = table[6:7].astype(jnp.int32) - anchor_y, cells_y
+            else:
+                along, length = table[5:6].astype(jnp.int32) - anchor_x, cells_x
+            there = picked(along, length)
+            pick = jnp.where(picked(table[7:8], depth), BF16(1), BF16(0))
+            both = jnp.concatenate(
+                [jnp.where(there, s, BF16(0)) for halves in parts for s in halves], axis=0
+            )
+            sums = sums_of(both, pick)
+            for f in range(5):
+                o = 2 * f * length
+                rim[b, f] = sums[o : o + length] + sums[o + length : o + 2 * length]
+        for f in range(5):
+            dep[f, :cells_y] += rim[0, f]
+            dep[f, cols - cells_y :] += rim[1, f]
 
     pl.semaphore_wait(barrier, len(everyone))
     sends = []
@@ -240,23 +273,26 @@
         )
     for send in sends:
         send.start()
-    deposit_stay((0, 1))
+    deposit_stay((4, 0, 1))
     for send in sends:
         send.wait()
-    deposit_got((4,))
-    loads[0].wait()
-    total = ener[...] + dep[4]
-    ener[...] = total
-    press[...] = (ADIABATIC_INDEX - 1.0) * total
+    deposit_got()
+    for b in range(FACES):
+        here = pl.ds(rows + b * move, move)
+        state_out[:, here] = got[b, :5]
+        cell_out[:, here] = got[b, 5:].astype(jnp.int32)
+    loads[4].wait()
+    y = row_iota((cells_y, depth))
     for x in range(cells_x):
-        side[0, pl.ds(x, 1)] = press[pl.ds(x * cells_y, 1)]
-        side[1, pl.ds(x, 1)] = press[pl.ds(x * cells_y + cells_y - 1, 1)]
-    outs = [
-        pltpu.make_async_copy(ener, energy_out, store_sem.at[0]),
-        pltpu.make_async_copy(got, arrived_out, store_sem.at[1]),
-    ]
-    for out in outs:
-        out.start()
+        here = pl.ds(x * cells_y, cells_y)
+        edge = jnp.where(y == 0, rim[2, 4, x : x + 1], 0.0)
+        edge += jnp.where(y == cells_y - 1, rim[3, 4, x : x + 1], 0.0)
+        total = ener[here] + (dep[4, here] + edge)
+        ener[here] = total
+        p = (ADIABATIC_INDEX - 1.0) * total
+        press[here] = p
+        side[0, pl.ds(x, 1)] = p[:1]
+        side[1, pl.ds(x, 1)] = p[cells_y - 1 :]
     faces = [
         press.at[pl.ds(0, cells_y)],
         press.at[pl.ds(cols - cells_y, cells_y)],
@@ -277,9 +313,8 @@
         )
     for send in sides:
         send.start()
-    deposit_got((0, 1, 2, 3))
     deposit_stay((2, 3))
-    for load in loads[1:]:
+    for load in loads[5:]:
         load.wait()
     for send in sides:
         send.wait()
@@ -289,7 +324,6 @@
     low_y = jnp.where(j > 0, halo[2], 0.0)
     high_y = jnp.where(j < ny - 1, halo[3], 0.0)
     z = lane_iota((cells_y, depth))
-    y = row_iota((cells_y, depth))
     fastest = jnp.zeros((cells_y, depth), F32)
     for x in range(cells_x):
         here = pl.ds(x * cells_y, cells_y)
@@ -300,21 +334,21 @@
         above = jnp.where(y == cells_y - 1, high_y[x : x + 1], pltpu.roll(p, cells_y - 1, axis=0))
         under = jnp.where(z == 0, 0.0, pltpu.roll(p, 1, axis=1))
         over = jnp.where(z == depth - 1, 0.0, pltpu.roll(p, depth - 1, axis=1))
-        rho = dens[here] + dep[0, here]
+
+        def deposited(f):
+            edge = jnp.where(y == 0, rim[2, f, x : x + 1], 0.0)
+            edge += jnp.where(y == cells_y - 1, rim[3, f, x : x + 1], 0.0)
+            return dep[f, here] + edge
+
+        rho = dens[here] + deposited(0)
         dens[here] = rho
-        wave = jnp.zeros_like(p)
+        speed = jnp.zeros_like(p)
         for k, (a, b) in enumerate(((before, after), (below, above), (under, over))):
-            impulse = mom[k, here] + dep[k + 1, here] - KICK * (0.5 * (b - a))
+            impulse = mom[k, here] + deposited(k + 1) - KICK * (0.5 * (b - a))
             mom[k, here] = impulse
-            wave = jnp.maximum(wave, jnp.abs(impulse / rho))
-        wave = wave + jnp.sqrt(ADIABATIC_INDEX * p / rho)
+            speed = jnp.maximum(speed, jnp.abs(impulse))
+        wave = speed / rho + jnp.sqrt(ADIABATIC_INDEX * p / rho)
         fastest = jnp.maximum(fastest, wave)
-    late = [
-        pltpu.make_async_copy(mom, momentum_out, store_sem.at[2]),
-        pltpu.make_async_copy(dens, density_out, store_sem.at[3]),
-    ]
-    for out in late:
-        out.start()
     top = jnp.max(fastest, axis=0, keepdims=True)
     top = jnp.maximum(top[:, :128], top[:, 128:])
     for phase, peers in enumerate((first, second)):
@@ -338,55 +372,47 @@
         for q in range(len(peers)):
             top = jnp.maximum(top, best_in[phase, q])
     step_out[...] = COURANT / jnp.broadcast_to(jnp.max(top, axis=1, keepdims=True), (1, 128))
-    for out in outs + late:
-        out.wait()
 
 
 def on_device(density, momentum, energy, mass, velocity, temp, cell, count):
     cells_x, cells_y, depth = density.shape
     rows = mass.shape[0]
     move = rows // 16
+    slots = rows + FACES * move
     cols = cells_x * cells_y
     vmem = pl.BlockSpec(memory_space=VMEM)
-    anyspace = pl.BlockSpec(memory_space=ANY)
-    stay, bucket = pl.pallas_call(
-        functools.partial(sort_kernel, cells_x, cells_y),
-        name="sort_parcels",
-        out_shape=(
-            jax.ShapeDtypeStruct((8, rows), F32),
-            jax.ShapeDtypeStruct((FACES, 8, move), F32),
-        ),
-        in_specs=[vmem] * 4 + [pl.BlockSpec(memory_space=pltpu.SMEM)],
-        out_specs=(vmem, vmem),
-        compiler_params=pltpu.CompilerParams(vmem_limit_bytes=48 * 2**20),
-    )(mass.reshape(1, rows), velocity, temp.reshape(1, rows), cell, count)
+    far = pl.BlockSpec(memory_space=HBM)
     nx, ny = lax.axis_size("gx"), lax.axis_size("gy")
     field = jax.ShapeDtypeStruct((cols, depth), F32)
-    dens, mom, ener, arrived, step = pl.pallas_call(
-        functools.partial(main_kernel, nx, ny, cells_x, cells_y),
-        name="deposit_and_push",
+    dens, mom, ener, state, cells, step = pl.pallas_call(
+        functools.partial(fused_kernel, nx, ny, cells_x, cells_y),
+        name="spray_step",
         out_shape=(
             field,
             jax.ShapeDtypeStruct((3, cols, depth), F32),
             field,
-            jax.ShapeDtypeStruct((FACES, 8, move), F32),
+            jax.ShapeDtypeStruct((5, slots), F32),
+            jax.ShapeDtypeStruct((3, slots), jnp.int32),
             jax.ShapeDtypeStruct((1, 128), F32),
         ),
-        in_specs=[vmem, vmem, anyspace, anyspace, anyspace],
-        out_specs=(anyspace, anyspace, anyspace, anyspace, vmem),
+        in_specs=[far] * 4 + [pl.BlockSpec(memory_space=pltpu.SMEM)] + [far] * 3,
+        out_specs=(vmem,) * 6,
         scratch_shapes=[
-            VMEM((cols, depth), F32),
-            VMEM((3, cols, depth), F32),
-            VMEM((cols, depth), F32),
+            VMEM((1, rows), F32),
+            VMEM((3, rows), F32),
+            VMEM((1, rows), F32),
+            VMEM((3, rows), jnp.int32),
+            VMEM((8, rows), F32),
+            VMEM((FACES, 8, move), F32),
             VMEM((cols, depth), F32),
             VMEM((5, cols, depth), F32),
+            VMEM((FACES, 5, cells_y, depth), F32),
             VMEM((FACES, 8, move), F32),
             VMEM((2, cells_x, depth), F32),
             VMEM((FACES, cells_y, depth), F32),
             VMEM((2, 1, 128), F32),
             VMEM((2, 15, 1, 128), F32),
-            pltpu.SemaphoreType.DMA((3,)),
-            pltpu.SemaphoreType.DMA((4,)),
+            pltpu.SemaphoreType.DMA((7,)),
             pltpu.SemaphoreType.DMA((FACES,)),
             pltpu.SemaphoreType.DMA((FACES,)),
             pltpu.SemaphoreType.DMA((FACES,)),
@@ -395,22 +421,24 @@
             pltpu.SemaphoreType.DMA((2, 15)),
         ],
         compiler_params=pltpu.CompilerParams(
-            vmem_limit_bytes=56 * 2**20, collective_id=0, has_side_effects=True
+            vmem_limit_bytes=32 * 2**20, collective_id=0, has_side_effects=True
         ),
     )(
-        stay,
-        bucket,
+        mass.reshape(1, rows),
+        velocity,
+        temp.reshape(1, rows),
+        cell,
+        count,
         density.reshape(cols, depth),
         momentum.reshape(3, cols, depth),
         energy.reshape(cols, depth),
     )
-    table = jnp.concatenate([stay] + [arrived[h] for h in range(FACES)], axis=1)
     return (
         dens.reshape(density.shape),
         mom.reshape(momentum.shape),
         ener.reshape(energy.shape),
-        table[:5],
-        table[5:].astype(jnp.int32),
+        state,
+        cells,
         step[0, 0],
     )
 

time: 59.2 us -> 50.5 us (0.85)
  Pallas kernels: 44.3 us -> 37.7 us
  local copies, waits for them, and re-layouts: 11.1 us -> 10 us
  other arithmetic: 0.77 us -> 0 us
    pallas_call x2 -> x1, Pallas kernels: 44.3 us -> 37.7 us  [on_device(): pl.pallas_call(functools.partial(fused_kernel, nx, ny, cells_x, cells_y),...]
    convert_element_type x1 -> x0, other arithmetic: 0.77 us -> none  [on_device(): table[5:].astype(jnp.int32)]
    concatenate x1 -> x0, local copies, waits for them, and re-layouts: 0.72 us -> none  [on_device(): table = jnp.concatenate([stay] + [arrived[h] for h in range(FACES)], axis=1)]
    unnamed x27 -> x19, local copies, waits for them, and re-layouts: 10.3 us -> 10 us
where the time goes in v2:
time: 50.5 us; the launch traced here: 50.2 us
  Pallas kernels  37.7 us (75%)
  local copies, waits for them, and re-layouts  10 us (20%)
  between operations  2.47 us (5%)
    pallas_call x1, Pallas kernels, on_device(): pl.pallas_call(functools.partial(fused_kernel, nx, ny, cells_x, cells_y),...  37.7 us
    unnamed x19, local copies, waits for them, and re-layouts  10 us

profile of v2, /device:TPU:1, one launch (start us, length us, event | category | flops | bytes accessed | tf_op | source)
XLA Modules:
  0.0 50.2 jit_solution(3913929771026997920)
XLA Ops:
  1.3 0.0 copy-start
  1.3 1.1 %copy-done = f32[3,16,16,256]{3,2,1,0:T(8,128)S(1)} copy-done((f32[3,16,16,256]{3,2,1,0:T(8,128)S(1)}, f32[3,16,16,256]{3,2,1,0:T(8,128)}, u32[]{:S(2)}) %copy-start) | copy-done | bytes 786456
  2.4 0.0 copy-start.1
  2.4 0.9 %copy-done.1 = f32[16,16,256]{2,1,0:T(8,128)S(1)} copy-done((f32[16,16,256]{2,1,0:T(8,128)S(1)}, f32[16,16,256]{2,1,0:T(8,128)}, u32[]{:S(2)}) %copy-start.1) | copy-done | bytes 262168
  3.4 0.0 copy-start.2
  3.4 0.9 %copy-done.2 = f32[16,16,256]{2,1,0:T(8,128)S(1)} copy-done((f32[16,16,256]{2,1,0:T(8,128)S(1)}, f32[16,16,256]{2,1,0:T(8,128)}, u32[]{:S(2)}) %copy-start.2) | copy-done | bytes 262168
  4.3 0.0 copy-start.3
  4.3 0.9 %copy-done.3 = f32[3,8192]{1,0:T(4,128)S(1)} copy-done((f32[3,8192]{1,0:T(4,128)S(1)}, f32[3,8192]{1,0:T(4,128)}, u32[]{:S(2)}) %copy-start.3) | copy-done | bytes 98328
  5.2 0.0 copy-start.4
  5.2 0.9 %copy-done.4 = s32[3,8192]{1,0:T(4,128)S(1)} copy-done((s32[3,8192]{1,0:T(4,128)S(1)}, s32[3,8192]{1,0:T(4,128)}, u32[]{:S(2)}) %copy-start.4) | copy-done | bytes 98328
  6.1 0.0 copy-start.5
  6.1 0.8 %copy-done.5 = f32[8192]{0:T(1024)S(1)} copy-done((f32[8192]{0:T(1024)S(1)}, f32[8192]{0:T(1024)}, u32[]{:S(2)}) %copy-start.5) | copy-done | bytes 32792
  6.9 0.0 copy-start.6
  6.9 0.8 %copy-done.6 = f32[8192]{0:T(1024)S(1)} copy-done((f32[8192]{0:T(1024)S(1)}, f32[8192]{0:T(1024)}, u32[]{:S(2)}) %copy-start.6) | copy-done | bytes 32792
  7.6 37.7 %spray_step.1 = (f32[256,256]{1,0:T(8,128)S(1)}, f32[3,256,256]{2,1,0:T(8,128)S(1)}, f32[256,256]{1,0:T(8,128)S(1)}, f32[5,10240]{1,0:T(8,128)S(1)}, s32[3,10240]{1,0:T(4,128)S(1)}, /*index=5*/f32[1,128]{1,0:T(1,128)S(1)}) custom-call(f32[1,8192]{1,0:T(1,128)S(1)} %bitcast.16, f32[3,8192]{1,0:T(4,128)S(1)} %copy-done.3, f32[1,8192]{1,0:T(1,128)S(1)} %bitcast.17, ...), custom_call_target="tpu_custom_call" | custom-call | tf_op jit(solution)/shard_map/spray_step/pallas_call | solution.py:387
  45.3 0.7 %copy.21 = f32[16,16,256]{2,1,0:T(8,128)} copy(f32[16,16,256]{2,1,0:T(8,128)S(1)} %bitcast.13) | data formatting | bytes 524288
  46.0 0.9 %copy.22 = f32[3,16,16,256]{3,2,1,0:T(8,128)} copy(f32[3,16,16,256]{3,2,1,0:T(8,128)S(1)} %bitcast.11) | data formatting | bytes 1572864
  46.9 0.7 %copy.23 = f32[16,16,256]{2,1,0:T(8,128)} copy(f32[16,16,256]{2,1,0:T(8,128)S(1)} %bitcast.12) | data formatting | bytes 524288
  47.6 0.7 %copy.24 = f32[5,10240]{1,0:T(8,128)} copy(f32[5,10240]{1,0:T(8,128)S(1)} %get-tuple-element.27) | data formatting | bytes 409600
  48.3 0.7 %copy.25 = s32[3,10240]{1,0:T(4,128)} copy(s32[3,10240]{1,0:T(4,128)S(1)} %get-tuple-element.28) | data formatting | bytes 245760
Async XLA Ops:
  1.3 1.1 %copy-start = (f32[3,16,16,256]{3,2,1,0:T(8,128)S(1)}, f32[3,16,16,256]{3,2,1,0:T(8,128)}, u32[]{:S(2)}) copy-start(f32[3,16,16,256]{3,2,1,0:T(8,128)} %param.9) | copy-start | bytes 2359300
  2.4 0.9 %copy-start.1 = (f32[16,16,256]{2,1,0:T(8,128)S(1)}, f32[16,16,256]{2,1,0:T(8,128)}, u32[]{:S(2)}) copy-start(f32[16,16,256]{2,1,0:T(8,128)} %param.8) | copy-start | bytes 786436
  3.4 0.9 %copy-start.2 = (f32[16,16,256]{2,1,0:T(8,128)S(1)}, f32[16,16,256]{2,1,0:T(8,128)}, u32[]{:S(2)}) copy-start(f32[16,16,256]{2,1,0:T(8,128)} %param.10) | copy-start | bytes 786436
  4.3 0.9 %copy-start.3 = (f32[3,8192]{1,0:T(4,128)S(1)}, f32[3,8192]{1,0:T(4,128)}, u32[]{:S(2)}) copy-start(f32[3,8192]{1,0:T(4,128)} %vel.1) | copy-start | bytes 294916
  5.2 0.9 %copy-start.4 = (s32[3,8192]{1,0:T(4,128)S(1)}, s32[3,8192]{1,0:T(4,128)}, u32[]{:S(2)}) copy-start(s32[3,8192]{1,0:T(4,128)} %cell.1) | copy-start | bytes 294916
  6.1 0.8 %copy-start.5 = (f32[8192]{0:T(1024)S(1)}, f32[8192]{0:T(1024)}, u32[]{:S(2)}) copy-start(f32[8192]{0:T(1024)} %param.11) | copy-start | bytes 98308
  6.9 0.8 %copy-start.6 = (f32[8192]{0:T(1024)S(1)}, f32[8192]{0:T(1024)}, u32[]{:S(2)}) copy-start(f32[8192]{0:T(1024)} %param.13) | copy-start | bytes 98308

commit v3 on v2

--- a/solution.py
+++ b/solution.py
@@ -374,6 +374,22 @@
     step_out[...] = COURANT / jnp.broadcast_to(jnp.max(top, axis=1, keepdims=True), (1, 128))
 
 
+def write_kernel(*refs):
+    sem = refs[-1]
+    count = len(refs) // 2
+    copies = [
+        pltpu.make_async_copy(refs[n], refs[count + n], sem.at[n]) for n in range(count)
+    ]
+    for copy in copies:
+        copy.start()
+    for copy in copies:
+        copy.wait()
+
+
+def in_hbm(array):
+    return pltpu.with_memory_space_constraint(array, HBM)
+
+
 def on_device(density, momentum, energy, mass, velocity, temp, cell, count):
     cells_x, cells_y, depth = density.shape
     rows = mass.shape[0]
@@ -424,15 +440,25 @@
             vmem_limit_bytes=32 * 2**20, collective_id=0, has_side_effects=True
         ),
     )(
-        mass.reshape(1, rows),
-        velocity,
-        temp.reshape(1, rows),
-        cell,
+        in_hbm(mass.reshape(1, rows)),
+        in_hbm(velocity),
+        in_hbm(temp.reshape(1, rows)),
+        in_hbm(cell),
         count,
-        density.reshape(cols, depth),
-        momentum.reshape(3, cols, depth),
-        energy.reshape(cols, depth),
+        in_hbm(density.reshape(cols, depth)),
+        in_hbm(momentum.reshape(3, cols, depth)),
+        in_hbm(energy.reshape(cols, depth)),
     )
+    results = (dens, mom, ener, state, cells, step)
+    dens, mom, ener, state, cells, step = pl.pallas_call(
+        write_kernel,
+        name="write_results",
+        out_shape=tuple(jax.ShapeDtypeStruct(r.shape, r.dtype) for r in results),
+        in_specs=[vmem] * 6,
+        out_specs=(far,) * 6,
+        scratch_shapes=[pltpu.SemaphoreType.DMA((6,))],
+        compiler_params=pltpu.CompilerParams(vmem_limit_bytes=2**20),
+    )(*results)
     return (
         dens.reshape(density.shape),
         mom.reshape(momentum.shape),

time: 50.5 us -> 40.7 us (0.81)
  local copies, waits for them, and re-layouts: 10 us -> 0 us
  Pallas kernels: 37.7 us -> 39.3 us
  between operations: 2.47 us -> 1.29 us
    unnamed x19 -> x0, local copies, waits for them, and re-layouts: 10 us -> none
    pallas_call x0 -> x1, Pallas kernels: none -> 1.26 us  [on_device(): pl.pallas_call(write_kernel, name='write_results', out_shape=tuple((jax.S...]
where the time goes in v3:
time: 40.7 us; the launch traced here: 40.6 us
  Pallas kernels  39.3 us (97%)
  between operations  1.29 us (3%)
    pallas_call x1, Pallas kernels, on_device(): pl.pallas_call(functools.partial(fused_kernel, nx, ny, cells_x, cells_y),...  38 us
    pallas_call x1, Pallas kernels, on_device(): pl.pallas_call(write_kernel, name='write_results', out_shape=tuple((jax.S...  1.26 us

profile of v3, /device:TPU:1, one launch (start us, length us, event | category | flops | bytes accessed | tf_op | source)
XLA Modules:
  0.0 40.6 jit_solution(18243619256190820491)
XLA Ops:
  1.3 38.0 %spray_step.1 = (f32[256,256]{1,0:T(8,128)S(1)}, f32[3,256,256]{2,1,0:T(8,128)S(1)}, f32[256,256]{1,0:T(8,128)S(1)}, f32[5,10240]{1,0:T(8,128)S(1)}, s32[3,10240]{1,0:T(4,128)S(1)}, /*index=5*/f32[1,128]{1,0:T(1,128)S(1)}) custom-call(f32[1,8192]{1,0:T(1,128)} %bitcast.13, f32[3,8192]{1,0:T(4,128)} %vel.1, f32[1,8192]{1,0:T(1,128)} %bitcast.14, ...), custom_call_target="tpu_custom_call" | custom-call | tf_op jit(solution)/shard_map/spray_step/pallas_call | solution.py:403
  39.3 1.3 %write_results.1 = (f32[256,256]{1,0:T(8,128)}, f32[3,256,256]{2,1,0:T(8,128)}, f32[256,256]{1,0:T(8,128)}, f32[5,10240]{1,0:T(8,128)}, s32[3,10240]{1,0:T(4,128)}, /*index=5*/f32[1,128]{1,0:T(1,128)}) custom-call(f32[256,256]{1,0:T(8,128)S(1)} %get-tuple-element.18.refs_0_, f32[3,256,256]{2,1,0:T(8,128)S(1)} %get-tuple-element.19.refs_1_, ...), custom_call_target="tpu_custom_call" | custom-call | tf_op jit(solution)/shard_map/write_results/pallas_call | solution.py:453

commit v4 on v3

--- a/solution.py
+++ b/solution.py
@@ -14,6 +14,8 @@
 FACES = 4
 F32 = jnp.float32
 BF16 = jnp.bfloat16
+F8 = jnp.float8_e4m3fn
+LOW_SCALE = 2048.0
 MESH = pl.DeviceIdType.MESH
 VMEM = pltpu.VMEM
 HBM = pltpu.HBM
@@ -153,6 +155,7 @@
     up_x, down_x = lax.rem(i + 1, nx), lax.rem(i + nx - 1, nx)
     up_y, down_y = lax.rem(j + 1, ny), lax.rem(j + ny - 1, ny)
     near = [(down_x, j), (up_x, j), (i, down_y), (i, up_y)]
+    has = [i > 0, i < nx - 1, j > 0, j < ny - 1]
     half = ny // 2
     spot = lax.div(j, half) * nx + i
     lane = lax.rem(j, half)
@@ -164,11 +167,6 @@
     second = []
     for q in range(1, size_b):
         second.append((i, lax.div(j, half) * half + lax.rem(lane + q, size_b)))
-
-    barrier = pltpu.get_barrier_semaphore()
-    everyone = near + first + second
-    for peer in everyone:
-        pl.semaphore_signal(barrier, inc=1, device_id=peer, device_id_type=MESH)
 
     pairs = [
         (cell, cell_in),
@@ -184,6 +182,21 @@
     ]
     for load in loads:
         load.start()
+
+    barrier = pltpu.get_barrier_semaphore()
+    for peer in first + second:
+        pl.semaphore_signal(barrier, inc=1, device_id=peer, device_id_type=MESH)
+    for h in range(FACES):
+
+        @pl.when(has[h])
+        def _():
+            pl.semaphore_signal(barrier, inc=1, device_id=near[h], device_id_type=MESH)
+
+        @pl.when(jnp.logical_not(has[h]))
+        def _():
+            got[h] = jnp.zeros_like(got[h])
+            halo[h] = jnp.zeros_like(halo[h])
+
     dep[...] = jnp.zeros_like(dep)
     for load in loads[:4]:
         load.wait()
@@ -192,10 +205,7 @@
     sort_parcels(
         cells_x, cells_y, anchor_x, anchor_y, mass_in, vel_in, temp_in, cell_in, count, stay, bucket
     )
-    state_out[:, :rows] = stay[:5]
-    cell_out[:, :rows] = stay[5:].astype(jnp.int32)
-
-    def terms(table, fields):
+    def terms(table, fields, scale):
         v = table[1:4]
         t = table[4:5]
         boiled = table[0:1] / (0.5 + jnp.exp(4.0 - 2.0 * t))
@@ -208,7 +218,7 @@
             else:
                 s = boiled * (t + 0.5 * jnp.sum(v * v, axis=0, keepdims=True))
             high = s.astype(BF16)
-            low = (s - high.astype(F32)).astype(BF16)
+            low = ((s - high.astype(F32)) * scale).astype(BF16)
             parts.append((high, low))
         return parts
 
@@ -219,46 +229,56 @@
     def sums_of(both, pick):
         return lax.dot_general(both, pick, (((1,), (1,)), ((), ())), preferred_element_type=F32)
 
-    wide = 2 * move
+    wide = 4 * move
 
     def deposit_stay(fields):
         def body(c, carry):
             table = stay[:, pl.ds(pl.multiple_of(c * wide, wide), wide)]
-            parts = terms(table, fields)
+            parts = terms(table, fields, LOW_SCALE)
             local_x = table[5:6].astype(jnp.int32) - anchor_x
             local_y = table[6:7].astype(jnp.int32) - anchor_y
             there = picked(local_x * cells_y + local_y, cols)
             pick = jnp.where(picked(table[7:8], depth), BF16(1), BF16(0))
-            for f, halves in zip(fields, parts):
-                both = jnp.concatenate([jnp.where(there, s, BF16(0)) for s in halves], axis=0)
-                sums = sums_of(both, pick)
-                dep[f] += sums[:cols] + sums[cols:]
+            pick_low = pick.astype(F8)
+            for f, (high, low) in zip(fields, parts):
+                sums = sums_of(jnp.where(there, high, BF16(0)), pick)
+                rest = sums_of(jnp.where(there, low, BF16(0)).astype(F8), pick_low)
+                dep[f] += sums + rest * (1.0 / LOW_SCALE)
             return carry
 
         lax.fori_loop(0, rows // wide, body, 0)
 
-    def deposit_got():
-        for b in range(FACES):
-            table = got[b]
-            parts = terms(table, range(5))
-            if b < 2:
-                along, length = table[6:7].astype(jnp.int32) - anchor_y, cells_y
-            else:
-                along, length = table[5:6].astype(jnp.int32) - anchor_x, cells_x
-            there = picked(along, length)
-            pick = jnp.where(picked(table[7:8], depth), BF16(1), BF16(0))
-            both = jnp.concatenate(
-                [jnp.where(there, s, BF16(0)) for halves in parts for s in halves], axis=0
-            )
-            sums = sums_of(both, pick)
-            for f in range(5):
-                o = 2 * f * length
-                rim[b, f] = sums[o : o + length] + sums[o + length : o + 2 * length]
-        for f in range(5):
-            dep[f, :cells_y] += rim[0, f]
-            dep[f, cols - cells_y :] += rim[1, f]
-
-    pl.semaphore_wait(barrier, len(everyone))
+    def arrivals(table, dim, fields):
+        if dim == 0:
+            along, length = table[6:7].astype(jnp.int32) - anchor_y, cells_y
+        else:
+            along, length = table[5:6].astype(jnp.int32) - anchor_x, cells_x
+        there = picked(along, length)
+        pick = jnp.where(picked(table[7:8], depth), BF16(1), BF16(0))
+        parts = terms(table, fields, 1.0)
+        both = jnp.concatenate(
+            [jnp.where(there, s, BF16(0)) for halves in parts for s in halves], axis=0
+        )
+        sums = sums_of(both, pick)
+        found = []
+        for n in range(len(fields)):
+            o = 2 * n * length
+            found.append(sums[o : o + length] + sums[o + length : o + 2 * length])
+        return found
+
+    def start_all(copies, faces):
+        for h in faces:
+            pl.when(has[h])(copies[h].start)
+
+    def wait_all(copies, faces):
+        for h in faces:
+            pl.when(has[h])(copies[h].wait_send)
+            pl.when(has[h])(copies[h ^ 1].wait_recv)
+
+    present = len(first) + len(second)
+    for h in range(FACES):
+        present = present + has[h].astype(jnp.int32)
+    pl.semaphore_wait(barrier, present)
     sends = []
     for h in range(FACES):
         sends.append(
@@ -271,28 +291,17 @@
                 device_id_type=MESH,
             )
         )
-    for send in sends:
-        send.start()
+    start_all(sends, range(FACES))
     deposit_stay((4, 0, 1))
-    for send in sends:
-        send.wait()
-    deposit_got()
-    for b in range(FACES):
-        here = pl.ds(rows + b * move, move)
-        state_out[:, here] = got[b, :5]
-        cell_out[:, here] = got[b, 5:].astype(jnp.int32)
+    wait_all(sends, (0, 1))
+    for b, base in ((0, 0), (1, cols - cells_y)):
+        for f, found in enumerate(arrivals(got[b], 0, range(5))):
+            dep[f, base : base + cells_y] += found
     loads[4].wait()
-    y = row_iota((cells_y, depth))
     for x in range(cells_x):
-        here = pl.ds(x * cells_y, cells_y)
-        edge = jnp.where(y == 0, rim[2, 4, x : x + 1], 0.0)
-        edge += jnp.where(y == cells_y - 1, rim[3, 4, x : x + 1], 0.0)
-        total = ener[here] + (dep[4, here] + edge)
-        ener[here] = total
-        p = (ADIABATIC_INDEX - 1.0) * total
-        press[here] = p
-        side[0, pl.ds(x, 1)] = p[:1]
-        side[1, pl.ds(x, 1)] = p[cells_y - 1 :]
+        for n, y in enumerate((0, cells_y - 1)):
+            here = pl.ds(x * cells_y + y, 1)
+            side[n, pl.ds(x, 1)] = (ADIABATIC_INDEX - 1.0) * (ener[here] + dep[4, here])
     faces = [
         press.at[pl.ds(0, cells_y)],
         press.at[pl.ds(cols - cells_y, cells_y)],
@@ -311,18 +320,28 @@
                 device_id_type=MESH,
             )
         )
-    for send in sides:
-        send.start()
+    start_all(sides, (2, 3))
+    wait_all(sends, (2, 3))
+    for b in (2, 3):
+        for f, found in enumerate(arrivals(got[b], 1, range(5))):
+            rim[b - 2, f] = found
+    y = row_iota((cells_y, depth))
+    for x in range(cells_x):
+        here = pl.ds(x * cells_y, cells_y)
+        edge = jnp.where(y == 0, rim[0, 4, x : x + 1], 0.0)
+        edge += jnp.where(y == cells_y - 1, rim[1, 4, x : x + 1], 0.0)
+        total = ener[here] + (dep[4, here] + edge)
+        ener[here] = total
+        press[here] = (ADIABATIC_INDEX - 1.0) * total
+    start_all(sides, (0, 1))
+    gone = [arrivals(bucket[h], 1, (4,))[0] * (ADIABATIC_INDEX - 1.0) for h in (2, 3)]
     deposit_stay((2, 3))
     for load in loads[5:]:
         load.wait()
-    for send in sides:
-        send.wait()
-
-    low_x = jnp.where(i > 0, halo[0], 0.0)
-    high_x = jnp.where(i < nx - 1, halo[1], 0.0)
-    low_y = jnp.where(j > 0, halo[2], 0.0)
-    high_y = jnp.where(j < ny - 1, halo[3], 0.0)
+    wait_all(sides, range(FACES))
+
+    low_x, high_x = halo[0], halo[1]
+    low_y, high_y = halo[2] + gone[0], halo[3] + gone[1]
     z = lane_iota((cells_y, depth))
     fastest = jnp.zeros((cells_y, depth), F32)
     for x in range(cells_x):
@@ -336,8 +355,8 @@
         over = jnp.where(z == depth - 1, 0.0, pltpu.roll(p, depth - 1, axis=1))
 
         def deposited(f):
-            edge = jnp.where(y == 0, rim[2, f, x : x + 1], 0.0)
-            edge += jnp.where(y == cells_y - 1, rim[3, f, x : x + 1], 0.0)
+            edge = jnp.where(y == 0, rim[0, f, x : x + 1], 0.0)
+            edge += jnp.where(y == cells_y - 1, rim[1, f, x : x + 1], 0.0)
             return dep[f, here] + edge
 
         rho = dens[here] + deposited(0)
@@ -367,6 +386,14 @@
             )
         for copy in copies:
             copy.start()
+        if phase == 0:
+            state_out[:, :rows] = stay[:5]
+            cell_out[:, :rows] = stay[5:].astype(jnp.int32)
+        else:
+            for b in range(FACES):
+                here = pl.ds(rows + b * move, move)
+                state_out[:, here] = got[b, :5]
+                cell_out[:, here] = got[b, 5:].astype(jnp.int32)
         for copy in copies:
             copy.wait()
         for q in range(len(peers)):
@@ -422,7 +449,7 @@
             VMEM((FACES, 8, move), F32),
             VMEM((cols, depth), F32),
             VMEM((5, cols, depth), F32),
-            VMEM((FACES, 5, cells_y, depth), F32),
+            VMEM((2, 5, cells_x, depth), F32),
             VMEM((FACES, 8, move), F32),
             VMEM((2, cells_x, depth), F32),
             VMEM((FACES, cells_y, depth), F32),

time: 40.7 us -> 36.3 us (0.89)
  Pallas kernels: 39.3 us -> 34.9 us
    pallas_call x1, Pallas kernels: 38 us -> 33.7 us  [on_device(): pl.pallas_call(functools.partial(fused_kernel, nx, ny, cells_x, cells_y),...]
where the time goes in v4:
time: 36.3 us; the launch traced here: 36.2 us
  Pallas kernels  34.9 us (96%)
  between operations  1.29 us (4%)
    pallas_call x1, Pallas kernels, on_device(): pl.pallas_call(functools.partial(fused_kernel, nx, ny, cells_x, cells_y),...  33.7 us
    pallas_call x1, Pallas kernels, on_device(): pl.pallas_call(write_kernel, name='write_results', out_shape=tuple((jax.S...  1.26 us

profile of v4, /device:TPU:1, one launch (start us, length us, event | category | flops | bytes accessed | tf_op | source)
XLA Modules:
  0.0 36.2 jit_solution(12703829504030889489)
XLA Ops:
  1.3 33.7 %spray_step.1 = (f32[256,256]{1,0:T(8,128)S(1)}, f32[3,256,256]{2,1,0:T(8,128)S(1)}, f32[256,256]{1,0:T(8,128)S(1)}, f32[5,10240]{1,0:T(8,128)S(1)}, s32[3,10240]{1,0:T(4,128)S(1)}, /*index=5*/f32[1,128]{1,0:T(1,128)S(1)}) custom-call(f32[1,8192]{1,0:T(1,128)} %bitcast.13, f32[3,8192]{1,0:T(4,128)} %vel.1, f32[1,8192]{1,0:T(1,128)} %bitcast.14, ...), custom_call_target="tpu_custom_call" | custom-call | tf_op jit(solution)/shard_map/spray_step/pallas_call | solution.py:430
  35.0 1.3 %write_results.1 = (f32[256,256]{1,0:T(8,128)}, f32[3,256,256]{2,1,0:T(8,128)}, f32[256,256]{1,0:T(8,128)}, f32[5,10240]{1,0:T(8,128)}, s32[3,10240]{1,0:T(4,128)}, /*index=5*/f32[1,128]{1,0:T(1,128)}) custom-call(f32[256,256]{1,0:T(8,128)S(1)} %get-tuple-element.18.refs_0_, f32[3,256,256]{2,1,0:T(8,128)S(1)} %get-tuple-element.19.refs_1_, ...), custom_call_target="tpu_custom_call" | custom-call | tf_op jit(solution)/shard_map/write_results/pallas_call | solution.py:480

commit v5 on v4

--- a/solution.py
+++ b/solution.py
@@ -202,9 +202,6 @@
         load.wait()
 
     anchor_x, anchor_y = i * cells_x, j * cells_y
-    sort_parcels(
-        cells_x, cells_y, anchor_x, anchor_y, mass_in, vel_in, temp_in, cell_in, count, stay, bucket
-    )
     def terms(table, fields, scale):
         v = table[1:4]
         t = table[4:5]
@@ -229,11 +226,9 @@
     def sums_of(both, pick):
         return lax.dot_general(both, pick, (((1,), (1,)), ((), ())), preferred_element_type=F32)
 
-    wide = 4 * move
-
-    def deposit_stay(fields):
-        def body(c, carry):
-            table = stay[:, pl.ds(pl.multiple_of(c * wide, wide), wide)]
+    def deposit_stay(fields, wide):
+        def body(start):
+            table = stay[:, pl.ds(start, wide)]
             parts = terms(table, fields, LOW_SCALE)
             local_x = table[5:6].astype(jnp.int32) - anchor_x
             local_y = table[6:7].astype(jnp.int32) - anchor_y
@@ -244,9 +239,18 @@
                 sums = sums_of(jnp.where(there, high, BF16(0)), pick)
                 rest = sums_of(jnp.where(there, low, BF16(0)).astype(F8), pick_low)
                 dep[f] += sums + rest * (1.0 / LOW_SCALE)
+
+        return body
+
+    def deposit_loop(fields):
+        wide = 8 * move
+        body = deposit_stay(fields, wide)
+
+        def step(c, carry):
+            body(pl.multiple_of(c * wide, wide))
             return carry
 
-        lax.fori_loop(0, rows // wide, body, 0)
+        lax.fori_loop(0, rows // wide, step, 0)
 
     def arrivals(table, dim, fields):
         if dim == 0:
@@ -275,6 +279,13 @@
             pl.when(has[h])(copies[h].wait_send)
             pl.when(has[h])(copies[h ^ 1].wait_recv)
 
+    sort_parcels(
+        cells_x, cells_y, anchor_x, anchor_y, mass_in, vel_in, temp_in, cell_in, count, stay, bucket
+    )
+    wide = rows
+    for start in range(0, rows, wide):
+        deposit_stay((4,), wide)(start)
+
     present = len(first) + len(second)
     for h in range(FACES):
         present = present + has[h].astype(jnp.int32)
@@ -292,7 +303,7 @@
             )
         )
     start_all(sends, range(FACES))
-    deposit_stay((4, 0, 1))
+    deposit_loop((0, 1,))
     wait_all(sends, (0, 1))
     for b, base in ((0, 0), (1, cols - cells_y)):
         for f, found in enumerate(arrivals(got[b], 0, range(5))):
@@ -335,7 +346,7 @@
         press[here] = (ADIABATIC_INDEX - 1.0) * total
     start_all(sides, (0, 1))
     gone = [arrivals(bucket[h], 1, (4,))[0] * (ADIABATIC_INDEX - 1.0) for h in (2, 3)]
-    deposit_stay((2, 3))
+    deposit_loop((2, 3))
     for load in loads[5:]:
         load.wait()
     wait_all(sides, range(FACES))

time: 36.3 us -> 34.2 us (0.942)
  Pallas kernels: 34.9 us -> 32.8 us
    pallas_call x1, Pallas kernels: 33.7 us -> 31.6 us  [on_device(): pl.pallas_call(functools.partial(fused_kernel, nx, ny, cells_x, cells_y),...]
where the time goes in v5:
time: 34.2 us; the launch traced here: 34.1 us
  Pallas kernels  32.8 us (96%)
  between operations  1.29 us (4%)
    pallas_call x1, Pallas kernels, on_device(): pl.pallas_call(functools.partial(fused_kernel, nx, ny, cells_x, cells_y),...  31.6 us
    pallas_call x1, Pallas kernels, on_device(): pl.pallas_call(write_kernel, name='write_results', out_shape=tuple((jax.S...  1.26 us

profile of v5, /device:TPU:1, one launch (start us, length us, event | category | flops | bytes accessed | tf_op | source)
XLA Modules:
  0.0 34.1 jit_solution(2785934591525726229)
XLA Ops:
  1.3 31.6 %spray_step.1 = (f32[256,256]{1,0:T(8,128)S(1)}, f32[3,256,256]{2,1,0:T(8,128)S(1)}, f32[256,256]{1,0:T(8,128)S(1)}, f32[5,10240]{1,0:T(8,128)S(1)}, s32[3,10240]{1,0:T(4,128)S(1)}, /*index=5*/f32[1,128]{1,0:T(1,128)S(1)}) custom-call(f32[1,8192]{1,0:T(1,128)} %bitcast.13, f32[3,8192]{1,0:T(4,128)} %vel.1, f32[1,8192]{1,0:T(1,128)} %bitcast.14, ...), custom_call_target="tpu_custom_call" | custom-call | tf_op jit(solution)/shard_map/spray_step/pallas_call | solution.py:441
  32.9 1.3 %write_results.1 = (f32[256,256]{1,0:T(8,128)}, f32[3,256,256]{2,1,0:T(8,128)}, f32[256,256]{1,0:T(8,128)}, f32[5,10240]{1,0:T(8,128)}, s32[3,10240]{1,0:T(4,128)}, /*index=5*/f32[1,128]{1,0:T(1,128)}) custom-call(f32[256,256]{1,0:T(8,128)S(1)} %get-tuple-element.18.refs_0_, f32[3,256,256]{2,1,0:T(8,128)S(1)} %get-tuple-element.19.refs_1_, ...), custom_call_target="tpu_custom_call" | custom-call | tf_op jit(solution)/shard_map/write_results/pallas_call | solution.py:491

commit v6 on v5

--- a/solution.py
+++ b/solution.py
@@ -29,16 +29,36 @@
     return lax.broadcasted_iota(jnp.int32, shape, 1)
 
 
+def folded(row, parts):
+    width = row.shape[1] // parts
+    pieces = [
+        row[r : r + 1, k * width : (k + 1) * width]
+        for r in range(row.shape[0])
+        for k in range(parts)
+    ]
+    return jnp.concatenate(pieces, axis=0)
+
+
+def folded_left(fold, step):
+    width = fold.shape[1]
+    if step >= width:
+        return pltpu.roll(fold, 8 - step // width, axis=0)
+    near = pltpu.roll(fold, width - step, axis=1)
+    return jnp.where(lane_iota(fold.shape) >= width - step, pltpu.roll(near, 7, axis=0), near)
+
+
 def pack_left(cells, shift, steps):
     width = cells.shape[1]
+    part = shift.shape[1]
     for k in range(steps):
         step = 1 << k
-        coming = pltpu.roll(cells, width - step, axis=1)
-        coming_shift = pltpu.roll(shift, width - step, axis=1)
-        take = (coming_shift & step) != 0
-        leave = (shift & step) != 0
-        cells = jnp.where(take, coming, cells)
-        shift = jnp.where(take, coming_shift, jnp.where(leave, 0, shift))
+        coming_shift = folded_left(shift, step)
+        take = coming_shift & step
+        shift = jnp.where(take != 0, coming_shift, jnp.where((shift & step) != 0, 0, shift))
+        spread = jnp.concatenate(
+            [jnp.broadcast_to(take[r : r + 1], (8, part)) for r in range(8)], axis=1
+        )
+        cells = jnp.where(spread != 0, pltpu.roll(cells, width - step, axis=1), cells)
     return cells, shift
 
 
@@ -91,13 +111,16 @@
     shift = lane_iota((1, rows)) - overall
     target = heading * move + own
     shift = jnp.where(moves, shift + target * rows, 0)
-    packed, key = pack_left(record, jnp.broadcast_to(shift, (8, rows)), rows.bit_length() - 1)
+    packed, key = pack_left(record, folded(shift, 8), rows.bit_length() - 1)
 
     wide = FACES * move
+    eighth = wide // 8
     packed = packed[:, :wide]
-    slot = key[:, :wide] // rows
-    place = lane_iota((8, wide))
-    present = place < jnp.concatenate([counts[4:5]] * (wide // 128), axis=1)
+    lead = wide * 8 // rows
+    slot = folded(key[:lead], 8 // lead) // rows
+    place = row_iota((8, eighth)) * eighth + lane_iota((8, eighth))
+    movers = jnp.concatenate([counts[4:5]] * (eighth // 128), axis=1)
+    present = place < jnp.broadcast_to(movers, (8, eighth))
     for h in range(FACES):
         mine = present & (slot // move == h)
         gap = jnp.where(mine, place - (slot - h * move), 0)

time: 34.2 us -> 34 us (level)
  no operation moved by 1% of the time
where the time goes in v6:
time: 34 us; the launch traced here: 33.9 us
  Pallas kernels  32.6 us (96%)
  between operations  1.29 us (4%)
    pallas_call x1, Pallas kernels, on_device(): pl.pallas_call(functools.partial(fused_kernel, nx, ny, cells_x, cells_y),...  31.3 us
    pallas_call x1, Pallas kernels, on_device(): pl.pallas_call(write_kernel, name='write_results', out_shape=tuple((jax.S...  1.26 us

profile of v6, /device:TPU:1, one launch (start us, length us, event | category | flops | bytes accessed | tf_op | source)
XLA Modules:
  0.0 33.9 jit_solution(10315045124737150924)
XLA Ops:
  1.3 31.3 %spray_step.1 = (f32[256,256]{1,0:T(8,128)S(1)}, f32[3,256,256]{2,1,0:T(8,128)S(1)}, f32[256,256]{1,0:T(8,128)S(1)}, f32[5,10240]{1,0:T(8,128)S(1)}, s32[3,10240]{1,0:T(4,128)S(1)}, /*index=5*/f32[1,128]{1,0:T(1,128)S(1)}) custom-call(f32[1,8192]{1,0:T(1,128)} %bitcast.13, f32[3,8192]{1,0:T(4,128)} %vel.1, f32[1,8192]{1,0:T(1,128)} %bitcast.14, ...), custom_call_target="tpu_custom_call" | custom-call | tf_op jit(solution)/shard_map/spray_step/pallas_call | solution.py:464
  32.6 1.3 %write_results.1 = (f32[256,256]{1,0:T(8,128)}, f32[3,256,256]{2,1,0:T(8,128)}, f32[256,256]{1,0:T(8,128)}, f32[5,10240]{1,0:T(8,128)}, s32[3,10240]{1,0:T(4,128)}, /*index=5*/f32[1,128]{1,0:T(1,128)}) custom-call(f32[256,256]{1,0:T(8,128)S(1)} %get-tuple-element.18.refs_0_, f32[3,256,256]{2,1,0:T(8,128)S(1)} %get-tuple-element.19.refs_1_, ...), custom_call_target="tpu_custom_call" | custom-call | tf_op jit(solution)/shard_map/write_results/pallas_call | solution.py:514

commit v7 on v6

--- a/solution.py
+++ b/solution.py
@@ -325,7 +325,7 @@
                 device_id_type=MESH,
             )
         )
-    start_all(sends, range(FACES))
+    start_all(sends, (2, 3, 0, 1))
     deposit_loop((0, 1,))
     wait_all(sends, (0, 1))
     for b, base in ((0, 0), (1, cols - cells_y)):
@@ -355,21 +355,27 @@
             )
         )
     start_all(sides, (2, 3))
-    wait_all(sends, (2, 3))
-    for b in (2, 3):
-        for f, found in enumerate(arrivals(got[b], 1, range(5))):
-            rim[b - 2, f] = found
     y = row_iota((cells_y, depth))
-    for x in range(cells_x):
-        here = pl.ds(x * cells_y, cells_y)
-        edge = jnp.where(y == 0, rim[0, 4, x : x + 1], 0.0)
-        edge += jnp.where(y == cells_y - 1, rim[1, 4, x : x + 1], 0.0)
-        total = ener[here] + (dep[4, here] + edge)
-        ener[here] = total
-        press[here] = (ADIABATIC_INDEX - 1.0) * total
-    start_all(sides, (0, 1))
+    long_way = (j == half - 1) | (j == half)
+
+    def finish_energy():
+        wait_all(sends, (2, 3))
+        for b in (2, 3):
+            for f, found in enumerate(arrivals(got[b], 1, range(5))):
+                rim[b - 2, f] = found
+        for x in range(cells_x):
+            here = pl.ds(x * cells_y, cells_y)
+            edge = jnp.where(y == 0, rim[0, 4, x : x + 1], 0.0)
+            edge += jnp.where(y == cells_y - 1, rim[1, 4, x : x + 1], 0.0)
+            total = ener[here] + (dep[4, here] + edge)
+            ener[here] = total
+            press[here] = (ADIABATIC_INDEX - 1.0) * total
+        start_all(sides, (0, 1))
+
+    pl.when(jnp.logical_not(long_way))(finish_energy)
     gone = [arrivals(bucket[h], 1, (4,))[0] * (ADIABATIC_INDEX - 1.0) for h in (2, 3)]
     deposit_loop((2, 3))
+    pl.when(long_way)(finish_energy)
     for load in loads[5:]:
         load.wait()
     wait_all(sides, range(FACES))

time: 34 us -> 33.5 us (0.985)
  Pallas kernels: 32.6 us -> 32.1 us
    pallas_call x1, Pallas kernels: 31.3 us -> 30.8 us  [on_device(): pl.pallas_call(functools.partial(fused_kernel, nx, ny, cells_x, cells_y),...]
where the time goes in v7:
time: 33.5 us; the launch traced here: 33.4 us
  Pallas kernels  32.1 us (96%)
  between operations  1.29 us (4%)
    pallas_call x1, Pallas kernels, on_device(): pl.pallas_call(functools.partial(fused_kernel, nx, ny, cells_x, cells_y),...  30.8 us
    pallas_call x1, Pallas kernels, on_device(): pl.pallas_call(write_kernel, name='write_results', out_shape=tuple((jax.S...  1.26 us

profile of v7, /device:TPU:1, one launch (start us, length us, event | category | flops | bytes accessed | tf_op | source)
XLA Modules:
  0.0 33.4 jit_solution(4284798258660499655)
XLA Ops:
  1.3 30.8 %spray_step.1 = (f32[256,256]{1,0:T(8,128)S(1)}, f32[3,256,256]{2,1,0:T(8,128)S(1)}, f32[256,256]{1,0:T(8,128)S(1)}, f32[5,10240]{1,0:T(8,128)S(1)}, s32[3,10240]{1,0:T(4,128)S(1)}, /*index=5*/f32[1,128]{1,0:T(1,128)S(1)}) custom-call(f32[1,8192]{1,0:T(1,128)} %bitcast.13, f32[3,8192]{1,0:T(4,128)} %vel.1, f32[1,8192]{1,0:T(1,128)} %bitcast.14, ...), custom_call_target="tpu_custom_call" | custom-call | tf_op jit(solution)/shard_map/spray_step/pallas_call | solution.py:470
  32.1 1.3 %write_results.1 = (f32[256,256]{1,0:T(8,128)}, f32[3,256,256]{2,1,0:T(8,128)}, f32[256,256]{1,0:T(8,128)}, f32[5,10240]{1,0:T(8,128)}, s32[3,10240]{1,0:T(4,128)}, /*index=5*/f32[1,128]{1,0:T(1,128)}) custom-call(f32[256,256]{1,0:T(8,128)S(1)} %get-tuple-element.18.refs_0_, f32[3,256,256]{2,1,0:T(8,128)S(1)} %get-tuple-element.19.refs_1_, ...), custom_call_target="tpu_custom_call" | custom-call | tf_op jit(solution)/shard_map/write_results/pallas_call | solution.py:520
